TPU v7x, 256 devices: a whole 4x4x8 slice. The times are simulated.
256 devices in a mesh: dp: 2 (over z_lo), expert: 128 (over y, z_hi, x, core).
Axes of the slice: x: 4, y: 4, z: 8 (z_hi: 4, z_lo: 2; z = z_hi * 2 + z_lo), core: 2. Of those that a mesh axis runs over, the one named last changes fastest.
Arguments:
- tokens: bfloat16 [32768, 2880], P('expert'), may hold values from -2 to 2
- segment_ids: int32 [32768], P('expert'), may hold values from 0 to 255, never falling along the last dimension, each value on 1 to 512 neighbouring positions
- expert_ids: int32 [32768, 4], P('expert'), may hold values from 0 to 127, as said below
- attn_gain: float32 [2880], replicated, may hold values from 0.1 to 1.9
- sinks: float32 [32], P('dp'), may hold values from 2 to 5
- qkv_master: float32 [2560, 2880], P(('dp', 'expert')), may hold values from -0.109375 to 0.109375
- qkv_mom: float32 [2560, 2880], P(('dp', 'expert')), may hold values from -0.006 to 0.006
- qkv_var: float32 [2560, 2880], P(('dp', 'expert')), may hold values from 1e-08 to 1e-06
- qkv_grad: float32 [2560, 2880], P(('dp', 'expert')), may hold values from -0.06 to 0.06
- o_master: float32 [2048, 2880], P(('dp', 'expert')), may hold values from -0.125 to 0.125
- o_mom: float32 [2048, 2880], P(('dp', 'expert')), may hold values from -0.006 to 0.006
- o_var: float32 [2048, 2880], P(('dp', 'expert')), may hold values from 1e-08 to 1e-06
- o_grad: float32 [2048, 2880], P(('dp', 'expert')), may hold values from -0.06 to 0.06
- router_weight: bfloat16 [2880, 128], replicated, may hold values from -0.109375 to 0.109375
- router_bias: float32 [128], replicated, may hold values from -4 to 4
- mlp_gain: float32 [2880], replicated, may hold values from 0.1 to 1.9
Outputs:
- dispatched: bfloat16 [128, 128, 2, 8, 2880], P('expert', None, 'dp')
- gate_slots: bfloat16 [128, 128, 2, 8], P('expert', None, 'dp')
Inputs may be any that keep to these rules, and one draw needn't show every extreme that they name: `expert_ids`: each row names 4 different experts. In each aligned block of 128 rows no expert is named more than 8 times, and one expert, the same in every block of a draw, is named exactly 8 times in every block.
All inputs are finite; a program needn't handle non-finite values.
Results may differ from a plain program's by a relative error of at most 0.012.
The roundings to bfloat16 on the way count: a program that leaves them out, or rounds other values in their place, can miss the bound.
Values may be sent and summed in bfloat16 or wider, within the bound.
A program may use at most 128 MiB of HBM per device.

v0:
```python
import jax
import jax.numpy as jnp
from jax import lax
from jax.sharding import PartitionSpec as P

HEADS = 32
KV_HEADS = 4
HEAD_DIM = 64
WINDOW = 128


beta_one = 0.9
beta_two = 0.999
adam_step = 100
learn_rate = 0.02
adam_eps = 1e-08
norm_eps = 1e-05
rope_base = 150000.0
contract_rows = (((1,), (1,)), ((), ()))


def in_blocks(shard, dim, devices):
    before, after = (shard.shape[:dim], shard.shape[dim + 1 :])
    return jnp.moveaxis(shard.reshape(*before, devices, -1, *after), dim, 0)


def sent_and_summed(shard, axis, dim):
    devices = lax.axis_size(axis)
    tiles = lax.all_to_all(in_blocks(shard, dim, devices), axis, 0, 0, tiled=True)
    return jnp.sum(tiles.astype(jnp.float32), axis=0)


def adam_weights(master, moment, second_mom, gradient):
    moment_new = beta_one * moment + (1.0 - beta_one) * gradient
    second_new = beta_two * second_mom + (1.0 - beta_two) * gradient * gradient
    fix_one = 1.0 - beta_one**adam_step
    fix_two = 1.0 - beta_two**adam_step
    update = moment_new / fix_one / (jnp.sqrt(second_new / fix_two) + adam_eps)
    return (master - learn_rate * update).astype(jnp.bfloat16)


def rms_scale(values, gain_vec):
    mean_sq = jnp.mean(values * values, axis=-1, keepdims=True)
    return values * lax.rsqrt(mean_sq + norm_eps) * gain_vec


def rotate(values, positions):
    half_dim = values.shape[-1] // 2
    frequency = rope_base ** (-(jnp.arange(half_dim).astype(jnp.float32) * 2.0) / values.shape[-1])
    angles = positions[:, None] * frequency[None, :]
    cosine = jnp.cos(angles)[:, None, :]
    sine_vals = jnp.sin(angles)[:, None, :]
    first_half = values[..., :half_dim]
    second_half = values[..., half_dim:]
    return jnp.concatenate(
        [
            first_half * cosine - second_half * sine_vals,
            second_half * cosine + first_half * sine_vals,
        ],
        axis=-1,
    )


def attention(queries, key_rows, value_rows, segments, sink_logits):
    row_count = queries.shape[0]
    scale = queries.shape[-1] ** (-0.5)
    scores = (
        jnp.einsum("tgrd,ugd->grtu", queries, key_rows, preferred_element_type=jnp.float32) * scale
    )
    position = jnp.arange(row_count, dtype=jnp.int32)
    offset = position[:, None] - position[None, :]
    allowed = (segments[:, None] == segments[None, :]) & (offset >= 0) & (offset < WINDOW)
    weights = jnp.where(allowed, jnp.exp(scores), 0.0)
    sink_terms = jnp.exp(sink_logits).reshape(key_rows.shape[1], -1)[:, :, None]
    running = sink_terms + jnp.sum(weights, axis=-1)
    attn_probs = (weights / running[..., None]).astype(jnp.bfloat16)
    attended = jnp.einsum(
        "grtu,ugd->tgrd", attn_probs, value_rows, preferred_element_type=jnp.float32
    )
    return attended.astype(jnp.bfloat16).reshape(row_count, -1)


def gate_values(logits, choices, experts):
    picked = choices[:, :, None] == jnp.arange(experts, dtype=jnp.int32)[None, None, :]
    chosen = jnp.sum(jnp.where(picked, logits[:, None, :], 0.0), axis=-1)
    raised = jnp.exp(chosen)
    return raised / jnp.sum(raised, axis=-1, keepdims=True)


def slot_targets(choices, capacity, experts):
    flat_ids = choices.reshape(-1)
    onehot = (flat_ids[:, None] == jnp.arange(experts, dtype=jnp.int32)[None, :]).astype(jnp.int32)
    earlier = jnp.cumsum(onehot, axis=0) - onehot
    slot_index = jnp.sum(earlier * onehot, axis=1)
    return flat_ids * capacity + slot_index


def on_device(
    tokens,
    segment_ids,
    expert_ids,
    attn_gain,
    sinks,
    qkv_master,
    qkv_mom,
    qkv_var,
    qkv_grad,
    o_master,
    o_mom,
    o_var,
    o_grad,
    router_weight,
    router_bias,
    mlp_gain,
):
    tok_rows = tokens.shape[0]
    width = tokens.shape[1]
    groups = lax.axis_size("dp")
    half_rows = tok_rows // groups
    group_index = lax.axis_index("dp")
    heads_here = sinks.shape[0]
    kv_here = KV_HEADS * heads_here // HEADS
    repeat_count = heads_here // kv_here
    q_rows = heads_here * HEAD_DIM
    kv_rows = kv_here * HEAD_DIM
    qkv_local = adam_weights(qkv_master, qkv_mom, qkv_var, qkv_grad)
    o_local = adam_weights(o_master, o_mom, o_var, o_grad)
    normed = rms_scale(tokens.astype(jnp.float32), attn_gain).astype(jnp.bfloat16)
    qkv_full, o_full = (
        lax.all_gather(qkv_local, "expert", axis=0, tiled=True),
        lax.all_gather(o_local, "expert", axis=0, tiled=True),
    )
    projected = lax.dot_general(normed, qkv_full, contract_rows, preferred_element_type=jnp.float32)
    positions = jnp.arange(tok_rows).astype(jnp.float32)
    queries = rotate(
        projected[:, :q_rows].reshape(tok_rows, heads_here, HEAD_DIM), positions
    ).astype(jnp.bfloat16)
    queries = queries.reshape(tok_rows, kv_here, repeat_count, HEAD_DIM)
    key_rows = rotate(
        projected[:, q_rows : q_rows + kv_rows].reshape(tok_rows, kv_here, HEAD_DIM), positions
    ).astype(jnp.bfloat16)
    value_rows = (
        projected[:, q_rows + kv_rows :].reshape(tok_rows, kv_here, HEAD_DIM).astype(jnp.bfloat16)
    )
    attended = attention(queries, key_rows, value_rows, segment_ids, sinks)
    update = jnp.dot(attended, o_full, preferred_element_type=jnp.float32)
    summed = sent_and_summed(update.astype(jnp.bfloat16), "dp", 0)
    own_rows = lax.dynamic_slice_in_dim(tokens, group_index * half_rows, half_rows, 0)
    own_choices = lax.dynamic_slice_in_dim(expert_ids, group_index * half_rows, half_rows, 0)
    residual = own_rows.astype(jnp.float32) + summed
    moe_in = rms_scale(residual, mlp_gain).astype(jnp.bfloat16)
    logits = jnp.dot(moe_in, router_weight, preferred_element_type=jnp.float32) + router_bias
    experts = router_weight.shape[1]
    top_count = expert_ids.shape[1]
    capacity = 2 * half_rows * top_count // experts
    gate_vals = gate_values(logits, own_choices, experts)
    target = slot_targets(own_choices, capacity, experts)
    matches = target[None, :] == jnp.arange(experts * capacity, dtype=jnp.int32)[:, None]
    token_match = jnp.any(matches.reshape(experts * capacity, half_rows, top_count), axis=2).astype(
        jnp.bfloat16
    )
    payload = jnp.dot(token_match, moe_in, preferred_element_type=jnp.float32).astype(jnp.bfloat16)
    slot_gates = jnp.sum(jnp.where(matches, gate_vals.reshape(-1)[None, :], 0.0), axis=1).astype(
        jnp.bfloat16
    )
    outgoing = (payload.reshape(experts, capacity, width), slot_gates.reshape(experts, capacity))
    got_rows, got_gates = (
        lax.all_to_all(outgoing[0], "expert", split_axis=0, concat_axis=0, tiled=True),
        lax.all_to_all(outgoing[1], "expert", split_axis=0, concat_axis=0, tiled=True),
    )
    sources = lax.axis_size("expert")
    per_device = experts // sources
    dispatched = jnp.transpose(
        got_rows.reshape(sources, per_device, capacity, width), (1, 0, 2, 3)
    )[:, :, None]
    gate_slots = jnp.transpose(got_gates.reshape(sources, per_device, capacity), (1, 0, 2))[
        :, :, None
    ]
    return (dispatched, gate_slots)


def solution(mesh):
    return jax.shard_map(
        on_device,
        mesh=mesh,
        in_specs=(
            P("expert", None),
            P("expert"),
            P("expert", None),
            P(),
            P("dp"),
            P(("dp", "expert"), None),
            P(("dp", "expert"), None),
            P(("dp", "expert"), None),
            P(("dp", "expert"), None),
            P(("dp", "expert"), None),
            P(("dp", "expert"), None),
            P(("dp", "expert"), None),
            P(("dp", "expert"), None),
            P(),
            P(),
            P(),
        ),
        out_specs=(P("expert", None, "dp", None, None), P("expert", None, "dp", None)),
        check_vma=False,
    )
```

profile of v0, /device:TPU:1, one launch (start us, length us, event | category | flops | bytes accessed | tf_op | source)
XLA Modules:
  0.0 429.5 jit_solution(17836636112195737621)
XLA Ops:
  7.2 2.0 fusion.41
  9.3 1.7 fusion.40
  11.1 0.7 exp.19
  11.8 0.1 add.101
  11.9 1.8 fusion.1
  13.7 0.2 multiply_cosine_fusion
  13.9 0.1 fusion.23
  14.0 100.6 %all-gather.6.cloned.1.call-done = bf16[128,10,2880]{2,1,0:T(8,128)(2,1)} async-done(((bf16[1,10,2880]{2,1,0:T(8,128)(2,1)}), bf16[128,10,2880]{2,1,0:T(8,128)(2,1)}) %all-gather.6.cloned.1.call-update) | async-done | bytes 7372816 | tf_op jit(solution)/shard_map/all_gather | solution.py:130
  114.7 14.4 %reshape.186 = bf16[1280,2880]{1,0:T(8,128)(2,1)} reshape(bf16[128,10,2880]{2,1,0:T(8,128)(2,1)} %all-gather.6.cloned.1.call-done) | data formatting | bytes 14745600
  129.0 5.9 %fusion.6 = f32[256,1280]{1,0:T(8,128)S(1)} fusion(bf16[1280,2880]{1,0:T(8,128)(2,1)} %reshape.186, bf16[256,2880]{0,1:T(8,128)(2,1)S(1)} %copy-done.1, f32[2880]{0:T(1024)S(1)} %copy-done.6, f32[256]{0:T(256)S(1)} %add_rsqrt_fusion), kind=kOutput, calls=%fused_computation.16 | convolution fusion | flops 1890385920 | bytes 10170624 | tf_op jit(solution)/shard_map/dot_general | solution.py:133
  135.0 1.1 slice.42
  136.1 2.6 copy.69
  138.7 0.1 copy.68
  138.8 0.1 copy.67
  138.9 1.4 subtract_convert_fusion
  140.3 1.1 fusion
  141.4 0.1 broadcast_add_fusion.1
  141.4 1.1 fusion.11
  142.5 59.9 %all-gather.4.cloned.1.call-done = bf16[1024,2880]{1,0:T(8,128)(2,1)} async-done(((bf16[8,2880]{1,0:T(8,128)(2,1)}), bf16[1024,2880]{1,0:T(8,128)(2,1)}) %all-gather.4.cloned.1.call-update) | async-done | bytes 5898256 | tf_op jit(solution)/shard_map/all_gather | solution.py:131
  202.4 5.2 %fusion.10 = bf16[360,2,8,128]{3,2,1,0:T(8,128)(2,1)S(1)} fusion(bf16[256,1024]{0,1:T(8,128)(2,1)S(1)} %bitcast.70, bf16[1024,2880]{1,0:T(8,128)(2,1)} %all-gather.4.cloned.1.call-done), kind=kOutput, calls=%fused_computation.23 | convolution fusion | flops 1510686720 | bytes 7897088 | tf_op jit(solution)/shard_map/dot_general | solution.py:146
  207.6 1.2 copy.84
  208.8 4.8 %all-to-all-start = ((bf16[2,128,2880]{1,2,0:T(8,128)(2,1)}), bf16[2,128,2880]{1,2,0:T(8,128)(2,1)}, u32[]{:S(2)}, u32[]{:S(2)}) async-start(bf16[2,128,2880]{1,2,0:T(8,128)(2,1)} %bitcast.60), calls=%async_computation | async-start | bytes 2949120 | tf_op jit(solution)/shard_map/all_to_all | solution.py:29
  213.6 0.1 copy.81
  213.7 0.1 eq.75
  213.8 0.1 eq.71
  213.9 0.1 copy.64
  214.0 0.2 fusion.20
  214.4 0.2 fusion.17
  214.6 0.1 reduce_sum.75
  214.7 0.1 copy.66
  214.8 0.4 fusion.4
  215.2 16.2 %all-to-all-done = bf16[2,128,2880]{1,2,0:T(8,128)(2,1)} async-done(((bf16[2,128,2880]{1,2,0:T(8,128)(2,1)}), bf16[2,128,2880]{1,2,0:T(8,128)(2,1)}, u32[]{:S(2)}, u32[]{:S(2)}) %all-to-all-start) | async-done | bytes 1474592 | tf_op jit(solution)/shard_map/all_to_all | solution.py:29
  231.4 1.8 convert_reduce_fusion
  233.3 0.4 multiply_reduce_fusion
  233.7 0.5 multiply_convert_fusion
  234.2 0.4 convolution_add_fusion
  234.6 0.2 select_reduce_fusion.1
  234.9 0.1 copy.74
  235.0 0.1 div.102
  235.1 0.3 select_reduce_fusion
  235.4 0.7 convert_element_type.127
  236.2 11.3 %all-to-all-start.2 = ((bf16[128,1,8]{2,1,0:T(2,128)(2,1)}), bf16[128,1,8]{2,1,0:T(2,128)(2,1)S(1)}, u32[]{:S(2)}, u32[]{:S(2)}) async-start(bf16[128,1,8]{2,1,0:T(2,128)(2,1)} %convert_element_type.127), calls=%async_computation.2 | async-start | bytes 131072 | tf_op jit(solution)/shard_map/all_to_all | solution.py:169
  247.4 4.3 convolution_convert_fusion
  251.7 8.5 %copy.72 = bf16[1024,2880]{1,0:T(8,128)(2,1)} copy(bf16[1024,2880]{0,1:T(8,128)(2,1)} %convolution_convert_fusion) | data formatting | bytes 11796480 | tf_op jit(solution)/shard_map/convert_element_type | solution.py:162
  260.2 14.2 %all-to-all-start.1 = ((bf16[128,8,2880]{2,1,0:T(8,128)(2,1)}), bf16[128,8,2880]{2,1,0:T(8,128)(2,1)}, u32[]{:S(2)}, u32[]{:S(2)}) async-start(bf16[128,8,2880]{2,1,0:T(8,128)(2,1)} %bitcast.59), calls=%async_computation.1 | async-start | bytes 12058624 | tf_op jit(solution)/shard_map/all_to_all | solution.py:168
  274.5 0.7 copy.76
  275.1 138.6 %all-to-all-done.1 = bf16[128,8,2880]{2,1,0:T(8,128)(2,1)} async-done(((bf16[128,8,2880]{2,1,0:T(8,128)(2,1)}), bf16[128,8,2880]{2,1,0:T(8,128)(2,1)}, u32[]{:S(2)}, u32[]{:S(2)}) %all-to-all-start.1) | async-done | bytes 5898272 | tf_op jit(solution)/shard_map/all_to_all | solution.py:168
  413.7 9.0 %copy.77 = bf16[1,128,1,8,2880]{1,4,3,2,0:T(8,128)(2,1)} copy(bf16[1,128,1,8,2880]{4,3,1,2,0:T(8,128)(2,1)} %bitcast.17) | data formatting | bytes 11796480
  (37 shorter events, 0.4 us)
Async XLA Ops:
  7.2 227.0 %copy-start = (bf16[2880,128]{1,0:T(8,128)(2,1)S(1)}, bf16[2880,128]{1,0:T(8,128)(2,1)}, u32[]{:S(2)}) copy-start(bf16[2880,128]{1,0:T(8,128)(2,1)} %param.29) | copy-start | bytes 2211844
  7.2 6.7 %copy-start.3 = (s32[256]{0:T(256)S(1)}, s32[256]{0:T(256)}, u32[]{:S(2)}) copy-start(s32[256]{0:T(256)} %param.17) | copy-start | bytes 3076
  7.2 107.5 %all-gather.6.cloned.1.call-start = ((), (), s32[]{:S(2)}) async-start(), calls=%async_computation.4 | async-start | bytes 12152832 | tf_op jit(solution)/shard_map/all_gather | solution.py:130
  9.3 193.1 %all-gather.4.cloned.1.call-start = ((), (), s32[]{:S(2)}) async-start(), calls=%async_computation.3 | async-start | bytes 6076416 | tf_op jit(solution)/shard_map/all_gather | solution.py:131
  14.0 115.1 %copy-start.1 = (bf16[256,2880]{0,1:T(8,128)(2,1)S(1)}, bf16[256,2880]{0,1:T(8,128)(2,1)}, u32[]{:S(2)}) copy-start(bf16[256,2880]{0,1:T(8,128)(2,1)} %param.16) | copy-start | bytes 4423684
  14.0 115.1 %copy-start.6 = (f32[2880]{0:T(1024)S(1)}, f32[2880]{0:T(1024)}, u32[]{:S(2)}) copy-start(f32[2880]{0:T(1024)} %param.19) | copy-start | bytes 34564
  207.6 6.0 %copy-start.4 = (s32[256,4]{0,1:T(4,128)S(1)}, s32[256,4]{0,1:T(4,128)}, u32[]{:S(2)}) copy-start(s32[256,4]{0,1:T(4,128)} %param.18) | copy-start | bytes 12292
  208.8 22.6 %all-to-all-start = ((bf16[2,128,2880]{1,2,0:T(8,128)(2,1)}), bf16[2,128,2880]{1,2,0:T(8,128)(2,1)}, u32[]{:S(2)}, u32[]{:S(2)}) async-start(bf16[2,128,2880]{1,2,0:T(8,128)(2,1)} %bitcast.60), calls=%async_computation | async-start | bytes 2949120 | tf_op jit(solution)/shard_map/all_to_all | solution.py:29
  214.4 19.3 %copy-start.2 = (f32[2880]{0:T(1024)S(1)}, f32[2880]{0:T(1024)}, u32[]{:S(2)}) copy-start(f32[2880]{0:T(1024)} %param.31) | copy-start | bytes 34564
  233.3 0.9 copy-start.5
  236.2 24.1 %all-to-all-start.2 = ((bf16[128,1,8]{2,1,0:T(2,128)(2,1)}), bf16[128,1,8]{2,1,0:T(2,128)(2,1)S(1)}, u32[]{:S(2)}, u32[]{:S(2)}) async-start(bf16[128,1,8]{2,1,0:T(2,128)(2,1)} %convert_element_type.127), calls=%async_computation.2 | async-start | bytes 131072 | tf_op jit(solution)/shard_map/all_to_all | solution.py:169
  260.2 153.4 %all-to-all-start.1 = ((bf16[128,8,2880]{2,1,0:T(8,128)(2,1)}), bf16[128,8,2880]{2,1,0:T(8,128)(2,1)}, u32[]{:S(2)}, u32[]{:S(2)}) async-start(bf16[128,8,2880]{2,1,0:T(8,128)(2,1)} %bitcast.59), calls=%async_computation.1 | async-start | bytes 12058624 | tf_op jit(solution)/shard_map/all_to_all | solution.py:168
Sparse Core Ops, SparseCore 0:
  12.0 102.6 all-gather.5
  118.2 84.1 all-gather.3
where the time goes:
time: 431 us; the launch traced here: 429 us
  waiting for transfers between devices  315 us (73%)
  local copies, waits for them, and re-layouts  40 us (9%)
  starting transfers between devices  30.3 us (7%)
  matrix products  18 us (4%)
  between operations  14.3 us (3%)
  other arithmetic  11.5 us (3%)
    all_to_all x1, waiting for transfers between devices, on_device(): lax.all_to_all(outgoing[0], 'expert', split_axis=0, concat_axis=0, tiled=...  139 us
    all_gather x1, waiting for transfers between devices, on_device(): lax.all_gather(qkv_local, 'expert', axis=0, tiled=True)  101 us
    all_gather x1, waiting for transfers between devices, on_device(): lax.all_gather(o_local, 'expert', axis=0, tiled=True)  59.9 us
    unnamed x18, local copies, waits for them, and re-layouts  23.5 us
    all_to_all x1, waiting for transfers between devices, sent_and_summed(): lax.all_to_all(in_blocks(shard, dim, devices), axis, 0, 0, tiled=True)  16.2 us
    all_to_all x1, starting transfers between devices, on_device(): lax.all_to_all(outgoing[0], 'expert', split_axis=0, concat_axis=0, tiled=...  14.2 us
    all_to_all x1, starting transfers between devices, on_device(): lax.all_to_all(outgoing[1], 'expert', split_axis=0, concat_axis=0, tiled=...  11.3 us
  transfers between devices with their start and end apart: 5, of which 4 were waited for; matrix products, arithmetic and copies ran while one was open for 11% of the time, Pallas kernels for 0%

commit v1 on v0

--- a/solution.py
+++ b/solution.py
@@ -1,13 +1,20 @@
 import jax
 import jax.numpy as jnp
+import numpy as np
 from jax import lax
+from jax.experimental import pallas as pl
+from jax.experimental.pallas import tpu as pltpu
 from jax.sharding import PartitionSpec as P
 
 HEADS = 32
 KV_HEADS = 4
 HEAD_DIM = 64
 WINDOW = 128
-
+WIDTH = 2880
+WIDE = 2944
+HALF = 1408
+META = 2816
+MESH = pl.DeviceIdType.MESH
 
 beta_one = 0.9
 beta_two = 0.999
@@ -17,17 +24,6 @@
 norm_eps = 1e-05
 rope_base = 150000.0
 contract_rows = (((1,), (1,)), ((), ()))
-
-
-def in_blocks(shard, dim, devices):
-    before, after = (shard.shape[:dim], shard.shape[dim + 1 :])
-    return jnp.moveaxis(shard.reshape(*before, devices, -1, *after), dim, 0)
-
-
-def sent_and_summed(shard, axis, dim):
-    devices = lax.axis_size(axis)
-    tiles = lax.all_to_all(in_blocks(shard, dim, devices), axis, 0, 0, tiled=True)
-    return jnp.sum(tiles.astype(jnp.float32), axis=0)
 
 
 def adam_weights(master, moment, second_mom, gradient):
@@ -87,12 +83,319 @@
     return raised / jnp.sum(raised, axis=-1, keepdims=True)
 
 
-def slot_targets(choices, capacity, experts):
+def slot_numbers(choices, experts):
     flat_ids = choices.reshape(-1)
     onehot = (flat_ids[:, None] == jnp.arange(experts, dtype=jnp.int32)[None, :]).astype(jnp.int32)
     earlier = jnp.cumsum(onehot, axis=0) - onehot
-    slot_index = jnp.sum(earlier * onehot, axis=1)
-    return flat_ids * capacity + slot_index
+    return jnp.sum(earlier * onehot, axis=1).reshape(choices.shape)
+
+
+def place():
+    e = lax.axis_index("expert")
+    core = lax.rem(e, 2)
+    x = lax.rem(lax.div(e, 2), 4)
+    z = lax.rem(lax.div(e, 8), 4)
+    y = lax.div(e, 32)
+    return e, y, z, x, core
+
+
+def expert_at(y, z, x, core):
+    return y * 32 + z * 8 + x * 2 + core
+
+
+def step(position, by):
+    return lax.rem(position + by, 4)
+
+
+def greet(peers):
+    barrier = pltpu.get_barrier_semaphore()
+    for peer in peers:
+        pl.semaphore_signal(barrier, inc=1, device_id={"expert": peer}, device_id_type=MESH)
+    pl.semaphore_wait(barrier, len(peers))
+
+
+def remote(src, dst, send_sem, recv_sem, peer):
+    return pltpu.make_async_remote_copy(
+        src_ref=src,
+        dst_ref=dst,
+        send_sem=send_sem,
+        recv_sem=recv_sem,
+        device_id={"expert": peer},
+        device_id_type=MESH,
+    )
+
+
+def gather_kernel(a, b, o, ga, gb, go, send, recv, pair_send, pair_recv, local):
+    _, y, z, x, core = place()
+    middle = y * (1 - core) + x * core
+    last = x * (1 - core) + y * core
+
+    def peer(last_at, middle_at, z_at):
+        return expert_at(
+            middle_at * (1 - core) + last_at * core,
+            z_at,
+            last_at * (1 - core) + middle_at * core,
+            core,
+        )
+
+    partner = expert_at(y, z, x, 1 - core)
+    ring = [
+        (peer(last, middle, step(z, 1)), peer(last, middle, step(z, 3))),
+        (peer(last, step(middle, 1), z), peer(last, step(middle, 3), z)),
+        (peer(step(last, 1), middle, z), peer(step(last, 3), middle, z)),
+    ]
+    greet([p for pair in ring for p in pair] + [partner])
+    streams = ((a, ga), (b, gb), (o, go))
+    up, down, far, far_two = 0, 1, 2, 3
+    sent, copies = [], {}
+
+    def go_on(s, stage, kind, src, dst, direction):
+        copy = remote(
+            src, dst, send.at[s, stage, kind], recv.at[s, stage, kind], ring[stage][direction]
+        )
+        copy.start()
+        copies[s, stage, kind] = copy
+        sent.append(copy)
+
+    def to_partner(s, k, block):
+        copy = remote(block, block, pair_send.at[s, k], pair_recv.at[s, k], partner)
+        copy.start()
+        copies[s, "pair", k] = copy
+        sent.append(copy)
+
+    own = []
+    for s, (shard, full) in enumerate(streams):
+        mine = full.at[core, last, middle, z]
+        go_on(s, 0, up, shard, mine, 0)
+        go_on(s, 0, down, shard, mine, 1)
+        copy = pltpu.make_async_copy(shard, mine, local.at[s])
+        copy.start()
+        own.append(copy)
+    for s, (_, full) in enumerate(streams):
+        if s < 2:
+            copies[s, 0, up].wait_recv()
+            block = full.at[core, last, middle, step(z, 3)]
+            go_on(s, 0, far, block, block, 0)
+        else:
+            copies[s, 0, down].wait_recv()
+            block = full.at[core, last, middle, step(z, 1)]
+            go_on(s, 0, far, block, block, 1)
+    for s, (_, full) in enumerate(streams):
+        copies[s, 0, down if s < 2 else up].wait_recv()
+        copies[s, 0, far].wait_recv()
+        own[s].wait()
+        block = full.at[core, last, middle]
+        go_on(s, 1, up, block, block, 0)
+        go_on(s, 1, down, block, block, 1)
+    for s, (_, full) in enumerate(streams):
+        copies[s, 1, up].wait_recv()
+        block = full.at[core, last, step(middle, 3), pl.ds(0, 2)]
+        go_on(s, 1, far, block, block, 0)
+        copies[s, 1, down].wait_recv()
+        block = full.at[core, last, step(middle, 1), pl.ds(2, 2)]
+        go_on(s, 1, far_two, block, block, 1)
+    for s, (_, full) in enumerate(streams):
+        copies[s, 1, far].wait_recv()
+        copies[s, 1, far_two].wait_recv()
+        block = full.at[core, last]
+        go_on(s, 2, up, block, block, 0)
+        go_on(s, 2, down, block, block, 1)
+        to_partner(s, 0, block)
+    for s, (_, full) in enumerate(streams):
+        copies[s, 2, up].wait_recv()
+        block = full.at[core, step(last, 3), pl.ds(0, 2)]
+        go_on(s, 2, far, block, block, 0)
+        to_partner(s, 1, full.at[core, step(last, 3)])
+        copies[s, 2, down].wait_recv()
+        block = full.at[core, step(last, 1), pl.ds(2, 2)]
+        go_on(s, 2, far_two, block, block, 1)
+        to_partner(s, 2, full.at[core, step(last, 1)])
+    for s, (_, full) in enumerate(streams):
+        copies[s, 2, far].wait_recv()
+        to_partner(s, 3, full.at[core, step(last, 2), pl.ds(0, 2)])
+        copies[s, 2, far_two].wait_recv()
+        to_partner(s, 4, full.at[core, step(last, 2), pl.ds(2, 2)])
+    for s in range(3):
+        for k in range(5):
+            copies[s, "pair", k].wait_recv()
+    for copy in sent:
+        copy.wait_send()
+
+
+def gather_weights(a, b, o):
+    return pl.pallas_call(
+        gather_kernel,
+        out_shape=[
+            jax.ShapeDtypeStruct((2, 4, 4, 4) + v.shape, jnp.bfloat16) for v in (a, b, o)
+        ],
+        in_specs=[pl.BlockSpec(memory_space=pltpu.VMEM)] * 3,
+        out_specs=[pl.BlockSpec(memory_space=pl.ANY)] * 3,
+        scratch_shapes=[
+            pltpu.SemaphoreType.DMA((3, 3, 4)),
+            pltpu.SemaphoreType.DMA((3, 3, 4)),
+            pltpu.SemaphoreType.DMA((3, 5)),
+            pltpu.SemaphoreType.DMA((3, 5)),
+            pltpu.SemaphoreType.DMA((3,)),
+        ],
+        compiler_params=pltpu.CompilerParams(collective_id=0, has_side_effects=True),
+        name="gather_weights",
+    )(a, b, o)
+
+
+def gathered_experts():
+    core, last, middle, z = np.meshgrid(
+        np.arange(2), np.arange(4), np.arange(4), np.arange(4), indexing="ij"
+    )
+    y = np.where(core == 0, middle, last)
+    x = np.where(core == 0, last, middle)
+    return (((y * 4 + z) * 4 + x) * 2 + core).reshape(-1)
+
+
+def dispatch_kernel(
+    rows, got, ring_rows, payload, picks, zsend, zrecv, send_sem, recv_sem
+):
+    _, y, z, x, core = place()
+    here = y * 8 + x * 2 + core
+    above, below = expert_at(y, step(z, 1), x, core), expert_at(y, step(z, 3), x, core)
+
+    def plane_expert(index):
+        return lax.div(index, 8) * 32 + z * 8 + lax.rem(index, 8)
+
+    barrier = pltpu.get_barrier_semaphore()
+    for peer in (above, below):
+        pl.semaphore_signal(barrier, inc=1, device_id={"expert": peer}, device_id_type=MESH)
+
+    def signal_one(i, carry):
+        peer = plane_expert(lax.rem(here + i, 32))
+        pl.semaphore_signal(barrier, inc=1, device_id={"expert": peer}, device_id_type=MESH)
+        return carry
+
+    lax.fori_loop(1, 32, signal_one, 0)
+    pl.semaphore_wait(barrier, 33)
+
+    meta, first, second = pl.ds(META, 128), pl.ds(0, HALF), pl.ds(HALF, META - HALF)
+    tail = pl.ds(HALF, WIDE - HALF)
+    sent = []
+
+    def pass_on(k, src, slot, lanes, peer):
+        copy = remote(
+            src.at[:, lanes], ring_rows.at[slot, :, lanes], zsend.at[k], zrecv.at[k], peer
+        )
+        copy.start()
+        sent.append(copy)
+        return copy
+
+    low_meta = pass_on(0, rows, 0, meta, above)
+    high_meta = pass_on(1, rows, 1, meta, below)
+    low_first = pass_on(2, rows, 0, first, above)
+    high_second = pass_on(3, rows, 1, second, below)
+    low_second = pass_on(4, rows, 0, second, above)
+    high_first = pass_on(5, rows, 1, first, below)
+
+    def choose(block, source):
+        data = source[:, META:WIDE].astype(jnp.float32)
+        code = lax.broadcasted_iota(jnp.int32, (128, 256), 1).astype(jnp.float32)
+        plane = z.astype(jnp.float32)
+        hit = jnp.zeros((128, 256), jnp.float32)
+        for k in range(4):
+            same = (data[:, 72 + k : 73 + k] == code) & (data[:, 76 + k : 77 + k] == plane)
+            hit = hit + jnp.where(same, 1.0, 0.0)
+        picks[block] = hit.T.astype(jnp.bfloat16)
+
+    def expand(block, source, start, tiles):
+        def one(i, carry):
+            lanes = pl.ds(pl.multiple_of(start + i * 128, 128), 128)
+            slots = jnp.dot(picks[block], source[:, lanes], preferred_element_type=jnp.float32)
+            payload[block, :, :, lanes] = slots.reshape(32, 8, 128).astype(jnp.bfloat16)
+            return carry
+
+        lax.fori_loop(0, tiles, one, 0)
+
+    def deliver(block, z_at, lanes):
+        row = expert_at(y, z_at, x, core)
+        pltpu.make_async_copy(
+            payload.at[block, here, :, lanes], got.at[row, :, lanes], recv_sem
+        ).start()
+
+        def one(i, carry):
+            index = lax.rem(here + i, 32)
+            remote(
+                payload.at[block, index, :, lanes],
+                got.at[row, :, lanes],
+                send_sem,
+                recv_sem,
+                plane_expert(index),
+            ).start()
+            return carry
+
+        lax.fori_loop(1, 32, one, 0)
+
+    choose(0, rows)
+    expand(0, rows, 0, 11)
+    deliver(0, z, first)
+    expand(0, rows, HALF, 12)
+    deliver(0, z, tail)
+    from_low, from_high, from_far = ring_rows.at[0], ring_rows.at[1], ring_rows.at[2]
+    low_meta.wait_recv()
+    far_meta = pass_on(6, from_low, 2, meta, above)
+    high_meta.wait_recv()
+    choose(1, from_low)
+    choose(2, from_high)
+    low_first.wait_recv()
+    far_first = pass_on(7, from_low, 2, first, above)
+    high_second.wait_recv()
+    far_second = pass_on(8, from_high, 2, second, below)
+    expand(1, from_low, 0, 11)
+    deliver(1, step(z, 3), first)
+    expand(2, from_high, HALF, 12)
+    deliver(2, step(z, 1), tail)
+    far_meta.wait_recv()
+    choose(3, from_far)
+    low_second.wait_recv()
+    expand(1, from_low, HALF, 12)
+    deliver(1, step(z, 3), tail)
+    high_first.wait_recv()
+    expand(2, from_high, 0, 11)
+    deliver(2, step(z, 1), first)
+    far_first.wait_recv()
+    expand(3, from_far, 0, 11)
+    deliver(3, step(z, 2), first)
+    far_second.wait_recv()
+    expand(3, from_far, HALF, 12)
+    deliver(3, step(z, 2), tail)
+    pltpu.make_async_copy(got, got, recv_sem).wait()
+    part = payload.at[:, pl.ds(0, 31)]
+    pltpu.make_async_copy(part, part, send_sem).wait()
+    for copy in sent:
+        copy.wait_send()
+
+
+def dispatch_rows(rows):
+    return pl.pallas_call(
+        dispatch_kernel,
+        out_shape=jax.ShapeDtypeStruct((128, 8, WIDE), jnp.bfloat16),
+        in_specs=[pl.BlockSpec(memory_space=pltpu.VMEM)],
+        out_specs=pl.BlockSpec(memory_space=pl.ANY),
+        scratch_shapes=[
+            pltpu.VMEM((3, 128, WIDE), jnp.bfloat16),
+            pltpu.VMEM((4, 32, 8, WIDE), jnp.bfloat16),
+            pltpu.VMEM((4, 256, 128), jnp.bfloat16),
+            pltpu.SemaphoreType.DMA((9,)),
+            pltpu.SemaphoreType.DMA((9,)),
+            pltpu.SemaphoreType.DMA,
+            pltpu.SemaphoreType.DMA,
+        ],
+        compiler_params=pltpu.CompilerParams(collective_id=1, has_side_effects=True),
+        name="dispatch_rows",
+    )(rows)
+
+
+def sent_and_summed(shard, axis, dim):
+    devices = lax.axis_size(axis)
+    before, after = (shard.shape[:dim], shard.shape[dim + 1 :])
+    blocks = jnp.moveaxis(shard.reshape(*before, devices, -1, *after), dim, 0)
+    tiles = lax.all_to_all(blocks, axis, 0, 0, tiled=True)
+    return jnp.sum(tiles.astype(jnp.float32), axis=0)
 
 
 def on_device(
@@ -114,10 +417,10 @@
     mlp_gain,
 ):
     tok_rows = tokens.shape[0]
-    width = tokens.shape[1]
     groups = lax.axis_size("dp")
     half_rows = tok_rows // groups
     group_index = lax.axis_index("dp")
+    expert_index = lax.axis_index("expert")
     heads_here = sinks.shape[0]
     kv_here = KV_HEADS * heads_here // HEADS
     repeat_count = heads_here // kv_here
@@ -125,12 +428,33 @@
     kv_rows = kv_here * HEAD_DIM
     qkv_local = adam_weights(qkv_master, qkv_mom, qkv_var, qkv_grad)
     o_local = adam_weights(o_master, o_mom, o_var, o_grad)
+    qkv_eight, qkv_two, o_full = gather_weights(qkv_local[:8], qkv_local[8:], o_local)
+    order = gathered_experts()
+    qkv_order = np.concatenate(
+        [
+            (order[:, None] * 10 + np.arange(8)[None, :]).reshape(-1),
+            (order[:, None] * 10 + np.arange(8, 10)[None, :]).reshape(-1),
+        ]
+    ).astype(np.int32)
+    o_order = (order[:, None] * 8 + np.arange(8)[None, :]).reshape(-1).astype(np.int32)
     normed = rms_scale(tokens.astype(jnp.float32), attn_gain).astype(jnp.bfloat16)
-    qkv_full, o_full = (
-        lax.all_gather(qkv_local, "expert", axis=0, tiled=True),
-        lax.all_gather(o_local, "expert", axis=0, tiled=True),
-    )
-    projected = lax.dot_general(normed, qkv_full, contract_rows, preferred_element_type=jnp.float32)
+    qkv_eight = qkv_eight.reshape(-1, WIDTH)
+    qkv_two = qkv_two.reshape(-1, WIDTH)
+    shuffled = jnp.concatenate(
+        [
+            lax.dot_general(normed, w, contract_rows, preferred_element_type=jnp.float32)
+            for w in (qkv_eight, qkv_two)
+        ],
+        axis=1,
+    )
+    high = lax.reduce_precision(shuffled, 8, 7)
+    parts = jnp.concatenate([high, shuffled - high], axis=0).astype(jnp.bfloat16)
+    width_here = q_rows + 2 * kv_rows
+    unshuffle = (
+        jnp.asarray(qkv_order)[:, None] == jnp.arange(width_here, dtype=jnp.int32)[None, :]
+    ).astype(jnp.bfloat16)
+    both = jnp.dot(parts, unshuffle, preferred_element_type=jnp.float32)
+    projected = both[:tok_rows] + both[tok_rows:]
     positions = jnp.arange(tok_rows).astype(jnp.float32)
     queries = rotate(
         projected[:, :q_rows].reshape(tok_rows, heads_here, HEAD_DIM), positions
@@ -143,7 +467,11 @@
         projected[:, q_rows + kv_rows :].reshape(tok_rows, kv_here, HEAD_DIM).astype(jnp.bfloat16)
     )
     attended = attention(queries, key_rows, value_rows, segment_ids, sinks)
-    update = jnp.dot(attended, o_full, preferred_element_type=jnp.float32)
+    shuffle = (
+        jnp.arange(q_rows, dtype=jnp.int32)[:, None] == jnp.asarray(o_order)[None, :]
+    ).astype(jnp.bfloat16)
+    attended = jnp.dot(attended, shuffle, preferred_element_type=jnp.float32).astype(jnp.bfloat16)
+    update = jnp.dot(attended, o_full.reshape(-1, WIDTH), preferred_element_type=jnp.float32)
     summed = sent_and_summed(update.astype(jnp.bfloat16), "dp", 0)
     own_rows = lax.dynamic_slice_in_dim(tokens, group_index * half_rows, half_rows, 0)
     own_choices = lax.dynamic_slice_in_dim(expert_ids, group_index * half_rows, half_rows, 0)
@@ -151,32 +479,27 @@
     moe_in = rms_scale(residual, mlp_gain).astype(jnp.bfloat16)
     logits = jnp.dot(moe_in, router_weight, preferred_element_type=jnp.float32) + router_bias
     experts = router_weight.shape[1]
-    top_count = expert_ids.shape[1]
-    capacity = 2 * half_rows * top_count // experts
-    gate_vals = gate_values(logits, own_choices, experts)
-    target = slot_targets(own_choices, capacity, experts)
-    matches = target[None, :] == jnp.arange(experts * capacity, dtype=jnp.int32)[:, None]
-    token_match = jnp.any(matches.reshape(experts * capacity, half_rows, top_count), axis=2).astype(
-        jnp.bfloat16
-    )
-    payload = jnp.dot(token_match, moe_in, preferred_element_type=jnp.float32).astype(jnp.bfloat16)
-    slot_gates = jnp.sum(jnp.where(matches, gate_vals.reshape(-1)[None, :], 0.0), axis=1).astype(
-        jnp.bfloat16
-    )
-    outgoing = (payload.reshape(experts, capacity, width), slot_gates.reshape(experts, capacity))
-    got_rows, got_gates = (
-        lax.all_to_all(outgoing[0], "expert", split_axis=0, concat_axis=0, tiled=True),
-        lax.all_to_all(outgoing[1], "expert", split_axis=0, concat_axis=0, tiled=True),
-    )
-    sources = lax.axis_size("expert")
-    per_device = experts // sources
-    dispatched = jnp.transpose(
-        got_rows.reshape(sources, per_device, capacity, width), (1, 0, 2, 3)
-    )[:, :, None]
-    gate_slots = jnp.transpose(got_gates.reshape(sources, per_device, capacity), (1, 0, 2))[
-        :, :, None
-    ]
-    return (dispatched, gate_slots)
+    gate_vals = gate_values(logits, own_choices, experts).astype(jnp.bfloat16)
+    slots = slot_numbers(own_choices, experts)
+    code = (own_choices // 32 * 8 + own_choices % 8) * 8 + slots
+    plane = own_choices // 8 % 4
+    extra = jnp.concatenate(
+        [
+            gate_vals,
+            own_choices.astype(jnp.bfloat16),
+            code.astype(jnp.bfloat16),
+            plane.astype(jnp.bfloat16),
+            jnp.zeros((half_rows, WIDE - WIDTH - 16), jnp.bfloat16),
+        ],
+        axis=1,
+    )
+    got = dispatch_rows(jnp.concatenate([moe_in, extra], axis=1))
+    dispatched = got[:, :, :WIDTH][None, :, None]
+    asked = got[:, :, WIDTH + 4 : WIDTH + 8].astype(jnp.float32) == expert_index.astype(jnp.float32)
+    gates = jnp.sum(
+        jnp.where(asked, got[:, :, WIDTH : WIDTH + 4].astype(jnp.float32), 0.0), axis=-1
+    ).astype(jnp.bfloat16)
+    return (dispatched, gates[None, :, None])
 
 
 def solution(mesh):

time: 431 us -> 237 us (0.55)
  waiting for transfers between devices: 315 us -> 14.8 us
  Pallas kernels: 0 us -> 157 us
  starting transfers between devices: 30.3 us -> 4.26 us
  between operations: 14.3 us -> 1.01 us
  local copies, waits for them, and re-layouts: 40 us -> 32.3 us
    all_gather x2 -> x0, waiting for transfers between devices: 161 us -> none  [the longest x1 101 us: on_device(): lax.all_gather(qkv_local, 'expert', axis=0, tiled=True)]
    pallas_call x0 -> x2, Pallas kernels: none -> 157 us  [the longest x1 93.8 us: dispatch_rows(): pl.pallas_call(dispatch_kernel, out_shape=jax.ShapeDtypeStruct((128, 8, W...]
    all_to_all x3 -> x1, waiting for transfers between devices: 155 us -> 14.8 us  [sent_and_summed(): tiles = lax.all_to_all(blocks, axis, 0, 0, tiled=True)]
    all_to_all x3 -> x1, starting transfers between devices: 30.2 us -> 4.26 us  [sent_and_summed(): tiles = lax.all_to_all(blocks, axis, 0, 0, tiled=True)]
    unnamed x18 -> x29, local copies, waits for them, and re-layouts: 23.5 us -> 12.5 us
    convert_element_type x2 -> x1, local copies, waits for them, and re-layouts: 9.25 us -> 0.14 us  [on_device(): gate_vals = gate_values(logits, own_choices, experts).astype(jnp.bfloat16)]
    broadcast_in_dim x0 -> x2, local copies, waits for them, and re-layouts: none -> 5.74 us  [the longest x1 5.73 us: on_device(): dispatched = got[:, :, :WIDTH][None, :, None]]
    reshape x1 -> x3, local copies, waits for them, and re-layouts: 1.21 us -> 5.74 us  [the longest x1 4.43 us: on_device(): qkv_two = qkv_two.reshape(-1, WIDTH)]
  transfers between devices with their start and end apart: 5 -> 1, of which waited for: 4 -> 1; matrix products, arithmetic and copies ran while one was open for 11% -> 2% of each run, Pallas kernels for 0% -> 0%
where the time goes in v1:
time: 237 us; the launch traced here: 236 us
  Pallas kernels  157 us (66%)
  local copies, waits for them, and re-layouts  32.3 us (14%)
  matrix products  16.8 us (7%)
  waiting for transfers between devices  14.8 us (6%)
  other arithmetic  10 us (4%)
  starting transfers between devices  4.26 us (2%)
    pallas_call x1, Pallas kernels, dispatch_rows(): pl.pallas_call(dispatch_kernel, out_shape=jax.ShapeDtypeStruct((128, 8, W...  93.8 us
    pallas_call x1, Pallas kernels, gather_weights(): pl.pallas_call(gather_kernel, out_shape=[jax.ShapeDtypeStruct((2, 4, 4, 4...  62.8 us
    all_to_all x1, waiting for transfers between devices, sent_and_summed(): tiles = lax.all_to_all(blocks, axis, 0, 0, tiled=True)  14.8 us
    unnamed x29, local copies, waits for them, and re-layouts  12.5 us
    dot_general x2, matrix products, on_device(): lax.dot_general(normed, w, contract_rows, preferred_element_type=jnp.floa...  6.38 us
    dot_general x1, matrix products, on_device(): jnp.dot(attended, o_full.reshape(-1, WIDTH), preferred_element_type=jnp.f...  5.88 us
    broadcast_in_dim x1, local copies, waits for them, and re-layouts, on_device(): dispatched = got[:, :, :WIDTH][None, :, None]  5.73 us
  transfers between devices with their start and end apart: 1, of which 1 were waited for; matrix products, arithmetic and copies ran while one was open for 2% of the time, Pallas kernels for 0%

profile of v1, /device:TPU:1, one launch (start us, length us, event | category | flops | bytes accessed | tf_op | source)
XLA Modules:
  0.0 235.9 jit_solution(10364225742107035155)
XLA Ops:
  0.7 1.4 fusion.39
  2.1 0.6 slice.66.b
  2.7 0.6 slice.65.a
  3.3 1.8 fusion.4
  5.1 1.7 fusion.48.o
  6.9 62.8 %gather_weights.1 = (bf16[2,4,4,4,8,2880]{5,4,3,2,1,0:T(8,128)(2,1)}, bf16[2,4,4,4,2,2880]{5,4,3,2,1,0:T(2,128)(2,1)}, bf16[2,4,4,4,8,2880]{5,4,3,2,1,0:T(8,128)(2,1)}) custom-call(bf16[8,2880]{1,0:T(8,128)(2,1)} %slice.65.a, bf16[2,2880]{1,0:T(2,128)(2,1)} %slice.66.b, bf16[8,2880]{1,0:T(8,128)(2,1)} %fusion.48.o), custom_call_target="tpu_custom_call" | custom-call | tf_op jit(solution)/shard_map/gather_weights/pallas_call | solution.py:226
  69.7 4.4 %reshape.150 = bf16[256,2880]{1,0:T(8,128)(2,1)} reshape(bf16[2,4,4,4,2,2880]{5,4,3,2,1,0:T(2,128)(2,1)} %get-tuple-element.6) | data formatting | bytes 2949120 | tf_op jit(solution)/shard_map/reshape | solution.py:442
  74.1 5.2 %fusion.22 = f32[256,1024]{1,0:T(8,128)S(1)} fusion(bf16[1024,2880]{1,0:T(8,128)(2,1)} %bitcast.71, bf16[256,2880]{0,1:T(8,128)(2,1)S(1)} %copy-done.2, f32[2880]{0:T(1024)S(1)} %copy-done.8, f32[256]{0:T(256)S(1)} %add_rsqrt_fusion), kind=kOutput, calls=%fused_computation.43 | convolution fusion | flops 1512898560 | bytes 8433920 | tf_op jit(solution)/shard_map/dot_general | solution.py:445
  79.3 1.2 fusion.20
  80.5 0.2 reduce-precision_convert_fusion
  80.7 2.1 fusion
  82.8 0.1 slice_add_fusion
  83.0 0.1 slice.73
  83.1 0.3 copy-done.9
  83.5 0.1 fusion.31
  83.7 0.1 copy.76
  83.8 0.3 copy.78
  84.2 0.2 multiply_cosine_fusion
  84.4 0.2 subtract_convert_fusion
  84.6 1.1 fusion.2
  85.8 1.1 fusion.14
  86.9 5.9 %fusion.9 = bf16[360,2,8,128]{3,2,1,0:T(8,128)(2,1)S(1)} fusion(bf16[1024,2880]{1,0:T(8,128)(2,1)} %bitcast.70, bf16[256,1024]{0,1:T(8,128)(2,1)S(1)} %bitcast.72, s32[1024]{0:T(1024)S(1)} %copy-done.11), kind=kOutput, calls=%fused_computation.24 | convolution fusion | flops 2048868352 | bytes 7901184 | tf_op jit(solution)/shard_map/dot_general | solution.py:474
  92.7 1.2 copy.101
  94.0 4.3 %all-to-all-start = ((bf16[2,128,2880]{1,2,0:T(8,128)(2,1)}), bf16[2,128,2880]{1,2,0:T(8,128)(2,1)S(1)}, u32[]{:S(2)}, u32[]{:S(2)}) async-start(bf16[2,128,2880]{1,2,0:T(8,128)(2,1)} %bitcast.60), calls=%async_computation | async-start | bytes 2949120 | tf_op jit(solution)/shard_map/all_to_all | solution.py:397
  98.2 0.1 copy.97
  98.4 0.1 eq.102
  98.6 0.1 copy.86
  98.7 0.2 fusion.26
  99.0 0.2 fusion.25
  99.2 0.1 reshape.157
  99.3 2.0 constant_dynamic-slice_fusion.1
  101.4 1.5 copy.98
  102.8 0.1 fusion.56
  103.0 14.8 %all-to-all-done = bf16[2,128,2880]{1,2,0:T(8,128)(2,1)S(1)} async-done(((bf16[2,128,2880]{1,2,0:T(8,128)(2,1)}), bf16[2,128,2880]{1,2,0:T(8,128)(2,1)S(1)}, u32[]{:S(2)}, u32[]{:S(2)}) %all-to-all-start) | async-done | bytes 1474592 | tf_op jit(solution)/shard_map/all_to_all | solution.py:397
  117.8 1.4 convert_reduce_fusion
  119.2 1.8 copy.82
  121.0 0.3 multiply_reduce_fusion
  121.4 0.2 multiply_convert_fusion
  121.6 0.9 copy-done.1
  122.5 0.4 convolution_add_fusion
  122.8 0.2 select_reduce_fusion.1
  123.1 0.1 copy.88
  123.3 2.0 concatenate.29.rows
  125.3 93.8 %dispatch_rows.1 = bf16[128,8,2944]{2,1,0:T(8,128)(2,1)} custom-call(bf16[128,2944]{1,0:T(8,128)(2,1)} %concatenate.29.rows), custom_call_target="tpu_custom_call" | custom-call | tf_op jit(solution)/shard_map/dispatch_rows/pallas_call | solution.py:374
  219.1 5.7 %slice_bitcast_fusion = bf16[1,128,1,8,2880]{4,3,1,2,0:T(8,128)(2,1)} fusion(bf16[128,8,2944]{2,1,0:T(8,128)(2,1)} %dispatch_rows.1), kind=kLoop, calls=%fused_computation.2 | loop fusion | bytes 11796480 | tf_op jit(solution)/shard_map/broadcast_in_dim | solution.py:497
  224.8 1.4 select_reduce_fusion
  226.2 9.0 %copy.89 = bf16[1,128,1,8,2880]{1,4,3,2,0:T(8,128)(2,1)} copy(bf16[1,128,1,8,2880]{4,3,1,2,0:T(8,128)(2,1)} %slice_bitcast_fusion) | data formatting | bytes 11796480
  235.2 0.7 copy.90
  (44 shorter events, 0.6 us)
Async XLA Ops:
  0.6 121.9 %copy-start = (bf16[2880,128]{1,0:T(8,128)(2,1)S(1)}, bf16[2880,128]{1,0:T(8,128)(2,1)}, u32[]{:S(2)}) copy-start(bf16[2880,128]{1,0:T(8,128)(2,1)} %param.31) | copy-start | bytes 2211844
  2.1 72.0 %copy-start.2 = (bf16[256,2880]{0,1:T(8,128)(2,1)S(1)}, bf16[256,2880]{0,1:T(8,128)(2,1)}, u32[]{:S(2)}) copy-start(bf16[256,2880]{0,1:T(8,128)(2,1)} %param.18) | copy-start | bytes 4423684
  2.1 72.0 %copy-start.8 = (f32[2880]{0:T(1024)S(1)}, f32[2880]{0:T(1024)}, u32[]{:S(2)}) copy-start(f32[2880]{0:T(1024)} %param.21) | copy-start | bytes 34564
  74.1 5.2 %copy-start.3 = (bf16[256,2880]{1,0:T(8,128)(2,1)S(1)}, bf16[256,2880]{1,0:T(8,128)(2,1)}, u32[]{:S(2)}) copy-start(bf16[256,2880]{1,0:T(8,128)(2,1)} %reshape.150) | copy-start | bytes 4423684
  79.3 1.4 copy-start.10
  82.8 0.7 copy-start.9
  82.8 0.7 copy-start.5
  85.8 1.1 copy-start.11
  92.7 5.5 %copy-start.6 = (s32[256,4]{0,1:T(4,128)S(1)}, s32[256,4]{0,1:T(4,128)}, u32[]{:S(2)}) copy-start(s32[256,4]{0,1:T(4,128)} %param.20) | copy-start | bytes 12292
  94.0 23.9 %all-to-all-start = ((bf16[2,128,2880]{1,2,0:T(8,128)(2,1)}), bf16[2,128,2880]{1,2,0:T(8,128)(2,1)S(1)}, u32[]{:S(2)}, u32[]{:S(2)}) async-start(bf16[2,128,2880]{1,2,0:T(8,128)(2,1)} %bitcast.60), calls=%async_computation | async-start | bytes 2949120 | tf_op jit(solution)/shard_map/all_to_all | solution.py:397
  119.2 2.2 copy-start.4
  121.0 1.5 copy-start.7
  121.6 0.9 copy-start.1

commit v2 on v1

--- a/solution.py
+++ b/solution.py
@@ -15,6 +15,8 @@
 HALF = 1408
 META = 2816
 MESH = pl.DeviceIdType.MESH
+GATHER_SPACE = pl.ANY
+FINISH_LANES = 768
 
 beta_one = 0.9
 beta_two = 0.999
@@ -125,7 +127,7 @@
     )
 
 
-def gather_kernel(a, b, o, ga, gb, go, send, recv, pair_send, pair_recv, local):
+def gather_kernel(a, b, o, ga, gb, go, send, recv, local):
     _, y, z, x, core = place()
     middle = y * (1 - core) + x * core
     last = x * (1 - core) + y * core
@@ -146,79 +148,103 @@
     ]
     greet([p for pair in ring for p in pair] + [partner])
     streams = ((a, ga), (b, gb), (o, go))
-    up, down, far, far_two = 0, 1, 2, 3
-    sent, copies = [], {}
-
-    def go_on(s, stage, kind, src, dst, direction):
-        copy = remote(
-            src, dst, send.at[s, stage, kind], recv.at[s, stage, kind], ring[stage][direction]
-        )
+    copies = {}
+
+    def move(s, tag, src, dst, to):
+        k = sum(1 for key in copies if key[0] == s)
+        copy = remote(src, dst, send.at[s, k], recv.at[s, k], to)
         copy.start()
-        copies[s, stage, kind] = copy
-        sent.append(copy)
-
-    def to_partner(s, k, block):
-        copy = remote(block, block, pair_send.at[s, k], pair_recv.at[s, k], partner)
-        copy.start()
-        copies[s, "pair", k] = copy
-        sent.append(copy)
+        copies[s, tag] = copy
+
+    def arrived(s, tag):
+        copies[s, tag].wait_recv()
+
+    fine = ((0, 0, 4), (3, 0, 4), (1, 0, 4), (2, 0, 2), (2, 2, 2))
+    coarse = (None,)
+    pieces = (fine, coarse, fine)
+
+    def part(s, last_by, k):
+        full = streams[s][1]
+        piece = pieces[s][k]
+        if piece is None:
+            return full.at[core, step(last, last_by)]
+        return full.at[core, step(last, last_by), step(middle, piece[0]), pl.ds(piece[1], piece[2])]
+
+    def along_last(s, k):
+        block = part(s, 0, k)
+        move(s, ("last", k, 0), block, block, ring[2][0])
+        move(s, ("last", k, 1), block, block, ring[2][1])
+        move(s, ("pair", 0, k), block, block, partner)
+
+    def from_last(s, k):
+        count = len(pieces[s])
+        low, high = part(s, 3, k), part(s, 1, k)
+        arrived(s, ("last", k, 0))
+        if k < 2 and count > 1:
+            move(s, ("far", k), low, low, ring[2][0])
+        move(s, ("pair", 3, k), low, low, partner)
+        arrived(s, ("last", k, 1))
+        if k >= 2 or count == 1:
+            move(s, ("far", k), high, high, ring[2][1])
+        move(s, ("pair", 1, k), high, high, partner)
 
     own = []
     for s, (shard, full) in enumerate(streams):
         mine = full.at[core, last, middle, z]
-        go_on(s, 0, up, shard, mine, 0)
-        go_on(s, 0, down, shard, mine, 1)
+        move(s, "z up", shard, mine, ring[0][0])
+        move(s, "z down", shard, mine, ring[0][1])
         copy = pltpu.make_async_copy(shard, mine, local.at[s])
         copy.start()
         own.append(copy)
     for s, (_, full) in enumerate(streams):
         if s < 2:
-            copies[s, 0, up].wait_recv()
+            arrived(s, "z up")
             block = full.at[core, last, middle, step(z, 3)]
-            go_on(s, 0, far, block, block, 0)
+            move(s, "z far", block, block, ring[0][0])
         else:
-            copies[s, 0, down].wait_recv()
+            arrived(s, "z down")
             block = full.at[core, last, middle, step(z, 1)]
-            go_on(s, 0, far, block, block, 1)
+            move(s, "z far", block, block, ring[0][1])
     for s, (_, full) in enumerate(streams):
-        copies[s, 0, down if s < 2 else up].wait_recv()
-        copies[s, 0, far].wait_recv()
+        arrived(s, "z down" if s < 2 else "z up")
+        arrived(s, "z far")
         own[s].wait()
         block = full.at[core, last, middle]
-        go_on(s, 1, up, block, block, 0)
-        go_on(s, 1, down, block, block, 1)
+        move(s, "middle up", block, block, ring[1][0])
+        move(s, "middle down", block, block, ring[1][1])
+        if s != 1:
+            along_last(s, 0)
     for s, (_, full) in enumerate(streams):
-        copies[s, 1, up].wait_recv()
+        arrived(s, "middle up")
         block = full.at[core, last, step(middle, 3), pl.ds(0, 2)]
-        go_on(s, 1, far, block, block, 0)
-        copies[s, 1, down].wait_recv()
+        move(s, "middle far 0", block, block, ring[1][0])
+        if s != 1:
+            along_last(s, 1)
+        arrived(s, "middle down")
         block = full.at[core, last, step(middle, 1), pl.ds(2, 2)]
-        go_on(s, 1, far_two, block, block, 1)
-    for s, (_, full) in enumerate(streams):
-        copies[s, 1, far].wait_recv()
-        copies[s, 1, far_two].wait_recv()
-        block = full.at[core, last]
-        go_on(s, 2, up, block, block, 0)
-        go_on(s, 2, down, block, block, 1)
-        to_partner(s, 0, block)
-    for s, (_, full) in enumerate(streams):
-        copies[s, 2, up].wait_recv()
-        block = full.at[core, step(last, 3), pl.ds(0, 2)]
-        go_on(s, 2, far, block, block, 0)
-        to_partner(s, 1, full.at[core, step(last, 3)])
-        copies[s, 2, down].wait_recv()
-        block = full.at[core, step(last, 1), pl.ds(2, 2)]
-        go_on(s, 2, far_two, block, block, 1)
-        to_partner(s, 2, full.at[core, step(last, 1)])
-    for s, (_, full) in enumerate(streams):
-        copies[s, 2, far].wait_recv()
-        to_partner(s, 3, full.at[core, step(last, 2), pl.ds(0, 2)])
-        copies[s, 2, far_two].wait_recv()
-        to_partner(s, 4, full.at[core, step(last, 2), pl.ds(2, 2)])
+        move(s, "middle far 1", block, block, ring[1][1])
+        if s != 1:
+            along_last(s, 2)
     for s in range(3):
-        for k in range(5):
-            copies[s, "pair", k].wait_recv()
-    for copy in sent:
+        arrived(s, "middle far 0")
+        if s != 1:
+            along_last(s, 3)
+        arrived(s, "middle far 1")
+        along_last(s, 4 if s != 1 else 0)
+    for k in range(5):
+        for s in range(3):
+            if k < len(pieces[s]):
+                from_last(s, k)
+    for k in range(5):
+        for s in range(3):
+            if k < len(pieces[s]):
+                block = part(s, 2, k)
+                arrived(s, ("far", k))
+                move(s, ("pair", 2, k), block, block, partner)
+    for (s, tag), copy in copies.items():
+        if tag[0] == "pair":
+            copy.wait_recv()
+    for copy in copies.values():
         copy.wait_send()
 
 
@@ -229,12 +255,10 @@
             jax.ShapeDtypeStruct((2, 4, 4, 4) + v.shape, jnp.bfloat16) for v in (a, b, o)
         ],
         in_specs=[pl.BlockSpec(memory_space=pltpu.VMEM)] * 3,
-        out_specs=[pl.BlockSpec(memory_space=pl.ANY)] * 3,
+        out_specs=[pl.BlockSpec(memory_space=GATHER_SPACE)] * 3,
         scratch_shapes=[
-            pltpu.SemaphoreType.DMA((3, 3, 4)),
-            pltpu.SemaphoreType.DMA((3, 3, 4)),
-            pltpu.SemaphoreType.DMA((3, 5)),
-            pltpu.SemaphoreType.DMA((3, 5)),
+            pltpu.SemaphoreType.DMA((3, 42)),
+            pltpu.SemaphoreType.DMA((3, 42)),
             pltpu.SemaphoreType.DMA((3,)),
         ],
         compiler_params=pltpu.CompilerParams(collective_id=0, has_side_effects=True),
@@ -273,24 +297,29 @@
     lax.fori_loop(1, 32, signal_one, 0)
     pl.semaphore_wait(barrier, 33)
 
-    meta, first, second = pl.ds(META, 128), pl.ds(0, HALF), pl.ds(HALF, META - HALF)
-    tail = pl.ds(HALF, WIDE - HALF)
-    sent = []
+    meta = pl.ds(META, 128)
+    chunks = ((0, 768), (768, 768), (1536, 768), (2304, 512))
+    from_low, from_high, from_far = ring_rows.at[0], ring_rows.at[1], ring_rows.at[2]
 
     def pass_on(k, src, slot, lanes, peer):
         copy = remote(
             src.at[:, lanes], ring_rows.at[slot, :, lanes], zsend.at[k], zrecv.at[k], peer
         )
         copy.start()
-        sent.append(copy)
         return copy
 
-    low_meta = pass_on(0, rows, 0, meta, above)
-    high_meta = pass_on(1, rows, 1, meta, below)
-    low_first = pass_on(2, rows, 0, first, above)
-    high_second = pass_on(3, rows, 1, second, below)
-    low_second = pass_on(4, rows, 0, second, above)
-    high_first = pass_on(5, rows, 1, first, below)
+    def leg(n):
+        if n < 4:
+            up = pass_on(2 * n, rows, 0, pl.ds(*chunks[n]), above)
+            down = pass_on(2 * n + 1, rows, 1, pl.ds(*chunks[3 - n]), below)
+        else:
+            up = pass_on(2 * n, from_low, 2, pl.ds(*chunks[n - 4]), above)
+            down = pass_on(2 * n + 1, from_high, 2, pl.ds(*chunks[7 - n]), below)
+        return up, down
+
+    low_meta = pass_on(12, rows, 0, meta, above)
+    high_meta = pass_on(13, rows, 1, meta, below)
+    legs = [leg(0)]
 
     def choose(block, source):
         data = source[:, META:WIDE].astype(jnp.float32)
@@ -302,16 +331,14 @@
             hit = hit + jnp.where(same, 1.0, 0.0)
         picks[block] = hit.T.astype(jnp.bfloat16)
 
-    def expand(block, source, start, tiles):
-        def one(i, carry):
-            lanes = pl.ds(pl.multiple_of(start + i * 128, 128), 128)
+    def deliver(block, source, z_at, chunk):
+        start, lanes_here = chunks[chunk]
+        lanes_here = lanes_here if chunk < 3 else WIDE - start
+        for at in range(0, lanes_here, 384):
+            lanes = pl.ds(start + at, min(384, lanes_here - at))
             slots = jnp.dot(picks[block], source[:, lanes], preferred_element_type=jnp.float32)
-            payload[block, :, :, lanes] = slots.reshape(32, 8, 128).astype(jnp.bfloat16)
-            return carry
-
-        lax.fori_loop(0, tiles, one, 0)
-
-    def deliver(block, z_at, lanes):
+            payload[block, :, :, lanes] = slots.reshape(32, 8, -1).astype(jnp.bfloat16)
+        lanes = pl.ds(start, lanes_here)
         row = expert_at(y, z_at, x, core)
         pltpu.make_async_copy(
             payload.at[block, here, :, lanes], got.at[row, :, lanes], recv_sem
@@ -331,42 +358,30 @@
         lax.fori_loop(1, 32, one, 0)
 
     choose(0, rows)
-    expand(0, rows, 0, 11)
-    deliver(0, z, first)
-    expand(0, rows, HALF, 12)
-    deliver(0, z, tail)
-    from_low, from_high, from_far = ring_rows.at[0], ring_rows.at[1], ring_rows.at[2]
+    for chunk in range(4):
+        deliver(0, rows, z, chunk)
     low_meta.wait_recv()
-    far_meta = pass_on(6, from_low, 2, meta, above)
+    far_meta = pass_on(14, from_low, 2, meta, above)
     high_meta.wait_recv()
     choose(1, from_low)
     choose(2, from_high)
-    low_first.wait_recv()
-    far_first = pass_on(7, from_low, 2, first, above)
-    high_second.wait_recv()
-    far_second = pass_on(8, from_high, 2, second, below)
-    expand(1, from_low, 0, 11)
-    deliver(1, step(z, 3), first)
-    expand(2, from_high, HALF, 12)
-    deliver(2, step(z, 1), tail)
-    far_meta.wait_recv()
-    choose(3, from_far)
-    low_second.wait_recv()
-    expand(1, from_low, HALF, 12)
-    deliver(1, step(z, 3), tail)
-    high_first.wait_recv()
-    expand(2, from_high, 0, 11)
-    deliver(2, step(z, 1), first)
-    far_first.wait_recv()
-    expand(3, from_far, 0, 11)
-    deliver(3, step(z, 2), first)
-    far_second.wait_recv()
-    expand(3, from_far, HALF, 12)
-    deliver(3, step(z, 2), tail)
+    for n in range(6):
+        up, down = legs[n]
+        if n < 5:
+            up.wait_send()
+            down.wait_send()
+            legs.append(leg(n + 1))
+        if n == 3:
+            far_meta.wait_recv()
+            choose(3, from_far)
+        up.wait_recv()
+        deliver(*((1, from_low, step(z, 3), n) if n < 4 else (3, from_far, step(z, 2), n - 4)))
+        down.wait_recv()
+        deliver(*((2, from_high, step(z, 1), 3 - n) if n < 4 else (3, from_far, step(z, 2), 7 - n)))
     pltpu.make_async_copy(got, got, recv_sem).wait()
     part = payload.at[:, pl.ds(0, 31)]
     pltpu.make_async_copy(part, part, send_sem).wait()
-    for copy in sent:
+    for copy in (low_meta, high_meta, far_meta) + legs[5]:
         copy.wait_send()
 
 
@@ -380,14 +395,59 @@
             pltpu.VMEM((3, 128, WIDE), jnp.bfloat16),
             pltpu.VMEM((4, 32, 8, WIDE), jnp.bfloat16),
             pltpu.VMEM((4, 256, 128), jnp.bfloat16),
-            pltpu.SemaphoreType.DMA((9,)),
-            pltpu.SemaphoreType.DMA((9,)),
+            pltpu.SemaphoreType.DMA((15,)),
+            pltpu.SemaphoreType.DMA((15,)),
             pltpu.SemaphoreType.DMA,
             pltpu.SemaphoreType.DMA,
         ],
         compiler_params=pltpu.CompilerParams(collective_id=1, has_side_effects=True),
         name="dispatch_rows",
     )(rows)
+
+
+def finish_kernel(got, out, gates):
+    spot = pl.program_id(0)
+    lanes_here = got.shape[2]
+    halves = []
+    for part in range(2):
+        rows = got[part * 64 : part * 64 + 64].reshape(512, lanes_here)
+        source = lax.broadcasted_iota(jnp.int32, (512, 512), 0)
+        target = lax.broadcasted_iota(jnp.int32, (512, 512), 1)
+        pick = (source == (target & 63) * 8 + (target >> 6)).astype(jnp.bfloat16)
+        halves.append(
+            lax.dot_general(rows, pick, (((0,), (0,)), ((), ())), preferred_element_type=jnp.float32)
+        )
+    whole = []
+    for c in range(8):
+        cut = slice(c * 64, c * 64 + 64)
+        whole.append(jnp.concatenate([halves[0][:, cut], halves[1][:, cut]], axis=1))
+        out[c] = whole[c].astype(jnp.bfloat16)
+
+    @pl.when(spot == WIDTH // FINISH_LANES)
+    def _():
+        mine = lax.axis_index("expert").astype(jnp.float32)
+        first = WIDTH % FINISH_LANES
+        for c in range(8):
+            data = whole[c][first : first + 8]
+            asked = jnp.where(data[4:8] == mine, data[:4], 0.0)
+            gates[c : c + 1] = jnp.sum(asked, axis=0, keepdims=True)
+
+
+def finish(got):
+    return pl.pallas_call(
+        finish_kernel,
+        grid=(-(-WIDE // FINISH_LANES),),
+        out_shape=[
+            jax.ShapeDtypeStruct((8, WIDTH, 128), jnp.bfloat16),
+            jax.ShapeDtypeStruct((8, 128), jnp.float32),
+        ],
+        in_specs=[pl.BlockSpec((128, 8, FINISH_LANES), lambda i: (0, 0, i))],
+        out_specs=[
+            pl.BlockSpec((8, FINISH_LANES, 128), lambda i: (0, i, 0)),
+            pl.BlockSpec((8, 128), lambda i: (0, 0)),
+        ],
+        name="finish",
+    )(got)
 
 
 def sent_and_summed(shard, axis, dim):
@@ -420,7 +480,6 @@
     groups = lax.axis_size("dp")
     half_rows = tok_rows // groups
     group_index = lax.axis_index("dp")
-    expert_index = lax.axis_index("expert")
     heads_here = sinks.shape[0]
     kv_here = KV_HEADS * heads_here // HEADS
     repeat_count = heads_here // kv_here
@@ -494,12 +553,10 @@
         axis=1,
     )
     got = dispatch_rows(jnp.concatenate([moe_in, extra], axis=1))
-    dispatched = got[:, :, :WIDTH][None, :, None]
-    asked = got[:, :, WIDTH + 4 : WIDTH + 8].astype(jnp.float32) == expert_index.astype(jnp.float32)
-    gates = jnp.sum(
-        jnp.where(asked, got[:, :, WIDTH : WIDTH + 4].astype(jnp.float32), 0.0), axis=-1
-    ).astype(jnp.bfloat16)
-    return (dispatched, gates[None, :, None])
+    dispatched, gates = finish(got)
+    dispatched = jnp.transpose(dispatched, (2, 0, 1))[None, :, None]
+    gates = jnp.transpose(gates).astype(jnp.bfloat16)[None, :, None]
+    return (dispatched, gates)
 
 
 def solution(mesh):

time: 237 us -> 206 us (0.87)
  local copies, waits for them, and re-layouts: 32.3 us -> 17.1 us
  Pallas kernels: 157 us -> 144 us
    pallas_call x1, Pallas kernels: 93.8 us -> 76.1 us  [dispatch_rows(): pl.pallas_call(dispatch_kernel, out_shape=jax.ShapeDtypeStruct((128, 8, W...]
    unnamed x29 -> x27, local copies, waits for them, and re-layouts: 12.5 us -> 3 us
    pallas_call x0 -> x1, Pallas kernels: none -> 8.11 us  [finish(): pl.pallas_call(finish_kernel, grid=(-(-WIDE // FINISH_LANES),), out_shape...]
    broadcast_in_dim x1 -> x0, local copies, waits for them, and re-layouts: 5.73 us -> none  [on_device(): dispatched = got[:, :, :WIDTH][None, :, None]]
    pallas_call x1, Pallas kernels: 62.8 us -> 60.1 us  [gather_weights(): pl.pallas_call(gather_kernel, out_shape=[jax.ShapeDtypeStruct((2, 4, 4, 4...]
where the time goes in v2:
time: 206 us; the launch traced here: 205 us
  Pallas kernels  144 us (70%)
  local copies, waits for them, and re-layouts  17.1 us (8%)
  matrix products  15.6 us (8%)
  waiting for transfers between devices  14.5 us (7%)
  other arithmetic  8.57 us (4%)
  starting transfers between devices  4.01 us (2%)
    pallas_call x1, Pallas kernels, dispatch_rows(): pl.pallas_call(dispatch_kernel, out_shape=jax.ShapeDtypeStruct((128, 8, W...  76.1 us
    pallas_call x1, Pallas kernels, gather_weights(): pl.pallas_call(gather_kernel, out_shape=[jax.ShapeDtypeStruct((2, 4, 4, 4...  60.1 us
    all_to_all x1, waiting for transfers between devices, sent_and_summed(): tiles = lax.all_to_all(blocks, axis, 0, 0, tiled=True)  14.5 us
    pallas_call x1, Pallas kernels, finish(): pl.pallas_call(finish_kernel, grid=(-(-WIDE // FINISH_LANES),), out_shape...  8.11 us
    dot_general x1, matrix products, on_device(): jnp.dot(attended, o_full.reshape(-1, WIDTH), preferred_element_type=jnp.f...  5.88 us
    dot_general x2, matrix products, on_device(): lax.dot_general(normed, w, contract_rows, preferred_element_type=jnp.floa...  5.2 us
    reshape x1, local copies, waits for them, and re-layouts, on_device(): qkv_two = qkv_two.reshape(-1, WIDTH)  4.43 us
  transfers between devices with their start and end apart: 1, of which 1 were waited for; matrix products, arithmetic and copies ran while one was open for 2% of the time, Pallas kernels for 0%

profile of v2, /device:TPU:1, one launch (start us, length us, event | category | flops | bytes accessed | tf_op | source)
XLA Modules:
  0.0 205.1 jit_solution(13254798331244285045)
XLA Ops:
  0.7 1.5 fusion.39
  2.1 0.6 slice.53.a
  2.8 0.6 slice.54.b
  3.4 1.7 fusion.48.o
  5.1 60.1 %gather_weights.1 = (bf16[2,4,4,4,8,2880]{5,4,3,2,1,0:T(8,128)(2,1)}, bf16[2,4,4,4,2,2880]{5,4,3,2,1,0:T(2,128)(2,1)}, bf16[2,4,4,4,8,2880]{5,4,3,2,1,0:T(8,128)(2,1)}) custom-call(bf16[8,2880]{1,0:T(8,128)(2,1)} %slice.53.a, bf16[2,2880]{1,0:T(2,128)(2,1)} %slice.54.b, bf16[8,2880]{1,0:T(8,128)(2,1)} %fusion.48.o), custom_call_target="tpu_custom_call" | custom-call | tf_op jit(solution)/shard_map/gather_weights/pallas_call | solution.py:252
  65.3 4.4 %reshape.142 = bf16[256,2880]{1,0:T(8,128)(2,1)} reshape(bf16[2,4,4,4,2,2880]{5,4,3,2,1,0:T(2,128)(2,1)} %get-tuple-element.8) | data formatting | bytes 2949120 | tf_op jit(solution)/shard_map/reshape | solution.py:501
  69.7 0.4 fusion.4
  70.1 2.7 %fusion.20 = f32[256,256]{1,0:T(8,128)S(1)} fusion(bf16[256,2880]{1,0:T(8,128)(2,1)} %reshape.142, bf16[256,2880]{0,1:T(8,128)(2,1)S(1)} %copy-done.2, f32[2880]{0:T(1024)S(1)} %copy-done.8, f32[256]{0:T(256)S(1)} %add_rsqrt_fusion), kind=kOutput, calls=%fused_computation.39 | convolution fusion | flops 380436480 | bytes 3223808 | tf_op jit(solution)/shard_map/dot_general | solution.py:504
  72.9 2.5 %fusion.22 = f32[256,1024]{1,0:T(8,128)S(1)} fusion(bf16[1024,2880]{1,0:T(8,128)(2,1)S(1)} %bitcast.72, bf16[256,2880]{0,1:T(8,128)(2,1)S(1)} %copy-done.2, f32[2880]{0:T(1024)S(1)} %copy-done.8, f32[256]{0:T(256)S(1)} %add_rsqrt_fusion), kind=kOutput, calls=%fused_computation.40 | convolution fusion | flops 1512898560 | bytes 8433920 | tf_op jit(solution)/shard_map/dot_general | solution.py:504
  75.4 0.2 reduce-precision_convert_fusion
  75.5 0.5 copy-done.10
  76.0 2.1 %fusion = f32[512,1280]{1,0:T(8,128)S(1)} fusion(s32[1280]{0:T(1024)S(1)} %copy-done.10, bf16[256,1280]{1,0:T(8,128)(2,1)S(1)} %get-tuple-element.13, bf16[256,1280]{1,0:T(8,128)(2,1)S(1)} %get-tuple-element.12), kind=kOutput, calls=%fused_computation.1 | convolution fusion | flops 1681981440 | bytes 3937280 | tf_op jit(solution)/shard_map/dot_general | solution.py:515
  78.1 0.1 slice_add_fusion
  78.3 0.1 slice.61
  78.4 0.3 copy.72
  78.8 0.1 copy.71
  78.9 0.2 multiply_cosine_fusion
  79.1 0.2 subtract_convert_fusion
  79.3 0.1 fusion.31
  79.5 0.1 copy.70
  79.6 1.1 fusion.2
  80.8 1.1 fusion.14
  81.9 5.9 %fusion.9 = bf16[360,2,8,128]{3,2,1,0:T(8,128)(2,1)S(1)} fusion(bf16[1024,2880]{1,0:T(8,128)(2,1)} %bitcast.71, bf16[256,1024]{0,1:T(8,128)(2,1)S(1)} %bitcast.74, s32[1024]{0:T(1024)S(1)} %copy-done.11), kind=kOutput, calls=%fused_computation.23 | convolution fusion | flops 2048868352 | bytes 7901184 | tf_op jit(solution)/shard_map/dot_general | solution.py:533
  87.7 1.2 copy.93
  89.0 4.0 %all-to-all-start = ((bf16[2,128,2880]{1,2,0:T(8,128)(2,1)}), bf16[2,128,2880]{1,2,0:T(8,128)(2,1)S(1)}, u32[]{:S(2)}, u32[]{:S(2)}) async-start(bf16[2,128,2880]{1,2,0:T(8,128)(2,1)} %bitcast.62), calls=%async_computation | async-start | bytes 2949120 | tf_op jit(solution)/shard_map/all_to_all | solution.py:457
  93.0 0.1 copy.90
  93.1 0.1 eq.96
  93.2 0.1 eq.92
  93.3 2.0 constant_dynamic-slice_fusion.1
  95.4 1.5 copy.89
  96.8 0.1 copy.80
  96.9 0.2 fusion.26
  97.3 0.2 fusion.25
  97.5 0.1 reshape.149
  97.6 0.1 fusion.56
  97.8 14.5 %all-to-all-done = bf16[2,128,2880]{1,2,0:T(8,128)(2,1)S(1)} async-done(((bf16[2,128,2880]{1,2,0:T(8,128)(2,1)}), bf16[2,128,2880]{1,2,0:T(8,128)(2,1)S(1)}, u32[]{:S(2)}, u32[]{:S(2)}) %all-to-all-start) | async-done | bytes 1474592 | tf_op jit(solution)/shard_map/all_to_all | solution.py:457
  112.2 1.4 convert_reduce_fusion
  113.6 1.8 copy.76
  115.4 0.3 multiply_reduce_fusion
  115.8 0.2 multiply_convert_fusion
  116.0 0.9 copy-done.1
  116.9 0.4 convolution_add_fusion
  117.3 0.2 select_reduce_fusion
  117.5 0.1 copy.82
  117.7 2.0 concatenate.29.rows
  119.7 76.1 %dispatch_rows.1.got = bf16[128,8,2944]{2,1,0:T(8,128)(2,1)} custom-call(bf16[128,2944]{1,0:T(8,128)(2,1)} %concatenate.29.rows), custom_call_target="tpu_custom_call" | custom-call | tf_op jit(solution)/shard_map/dispatch_rows/pallas_call | solution.py:389
  195.7 8.1 %finish.1 = (bf16[8,2880,128]{2,1,0:T(8,128)(2,1)}, f32[8,128]{1,0:T(8,128)}) custom-call(bf16[128,8,2944]{2,1,0:T(8,128)(2,1)} %dispatch_rows.1.got), custom_call_target="tpu_custom_call" | custom-call | tf_op jit(solution)/shard_map/finish/pallas_call | solution.py:437
  203.8 1.3 convert_bitcast_fusion
  (42 shorter events, 0.4 us)
Async XLA Ops:
  0.6 116.3 %copy-start = (bf16[2880,128]{1,0:T(8,128)(2,1)S(1)}, bf16[2880,128]{1,0:T(8,128)(2,1)}, u32[]{:S(2)}) copy-start(bf16[2880,128]{1,0:T(8,128)(2,1)} %param.31) | copy-start | bytes 2211844
  0.6 69.0 %copy-start.2 = (bf16[256,2880]{0,1:T(8,128)(2,1)S(1)}, bf16[256,2880]{0,1:T(8,128)(2,1)}, u32[]{:S(2)}) copy-start(bf16[256,2880]{0,1:T(8,128)(2,1)} %param.18) | copy-start | bytes 4423684
  65.3 4.9 %copy-start.8 = (f32[2880]{0:T(1024)S(1)}, f32[2880]{0:T(1024)}, u32[]{:S(2)}) copy-start(f32[2880]{0:T(1024)} %param.21) | copy-start | bytes 34564
  69.7 3.2 %copy-start.7 = (bf16[2,4,4,4,8,2880]{5,4,3,2,1,0:T(8,128)(2,1)S(1)}, bf16[2,4,4,4,8,2880]{5,4,3,2,1,0:T(8,128)(2,1)}, u32[]{:S(2)}) copy-start(bf16[2,4,4,4,8,2880]{5,4,3,2,1,0:T(8,128)(2,1)} %get-tuple-element.7) | copy-start | bytes 17694724
  75.3 0.7 copy-start.10
  78.4 0.9 copy-start.4
  78.4 1.0 copy-start.9
  80.8 1.1 copy-start.11
  88.9 4.0 %copy-start.5 = (s32[256,4]{0,1:T(4,128)S(1)}, s32[256,4]{0,1:T(4,128)}, u32[]{:S(2)}) copy-start(s32[256,4]{0,1:T(4,128)} %param.20) | copy-start | bytes 12292
  89.0 23.3 %all-to-all-start = ((bf16[2,128,2880]{1,2,0:T(8,128)(2,1)}), bf16[2,128,2880]{1,2,0:T(8,128)(2,1)S(1)}, u32[]{:S(2)}, u32[]{:S(2)}) async-start(bf16[2,128,2880]{1,2,0:T(8,128)(2,1)} %bitcast.62), calls=%async_computation | async-start | bytes 2949120 | tf_op jit(solution)/shard_map/all_to_all | solution.py:457
  113.6 2.2 %copy-start.3 = (f32[2880]{0:T(1024)S(1)}, f32[2880]{0:T(1024)}, u32[]{:S(2)}) copy-start(f32[2880]{0:T(1024)} %param.33) | copy-start | bytes 34564
  115.4 1.5 copy-start.6
  116.0 0.9 copy-start.1

commit v3 on v2

--- a/solution.py
+++ b/solution.py
@@ -6,8 +6,6 @@
 from jax.experimental.pallas import tpu as pltpu
 from jax.sharding import PartitionSpec as P
 
-HEADS = 32
-KV_HEADS = 4
 HEAD_DIM = 64
 WINDOW = 128
 WIDTH = 2880
@@ -25,7 +23,6 @@
 adam_eps = 1e-08
 norm_eps = 1e-05
 rope_base = 150000.0
-contract_rows = (((1,), (1,)), ((), ()))
 
 
 def adam_weights(master, moment, second_mom, gradient):
@@ -35,61 +32,6 @@
     fix_two = 1.0 - beta_two**adam_step
     update = moment_new / fix_one / (jnp.sqrt(second_new / fix_two) + adam_eps)
     return (master - learn_rate * update).astype(jnp.bfloat16)
-
-
-def rms_scale(values, gain_vec):
-    mean_sq = jnp.mean(values * values, axis=-1, keepdims=True)
-    return values * lax.rsqrt(mean_sq + norm_eps) * gain_vec
-
-
-def rotate(values, positions):
-    half_dim = values.shape[-1] // 2
-    frequency = rope_base ** (-(jnp.arange(half_dim).astype(jnp.float32) * 2.0) / values.shape[-1])
-    angles = positions[:, None] * frequency[None, :]
-    cosine = jnp.cos(angles)[:, None, :]
-    sine_vals = jnp.sin(angles)[:, None, :]
-    first_half = values[..., :half_dim]
-    second_half = values[..., half_dim:]
-    return jnp.concatenate(
-        [
-            first_half * cosine - second_half * sine_vals,
-            second_half * cosine + first_half * sine_vals,
-        ],
-        axis=-1,
-    )
-
-
-def attention(queries, key_rows, value_rows, segments, sink_logits):
-    row_count = queries.shape[0]
-    scale = queries.shape[-1] ** (-0.5)
-    scores = (
-        jnp.einsum("tgrd,ugd->grtu", queries, key_rows, preferred_element_type=jnp.float32) * scale
-    )
-    position = jnp.arange(row_count, dtype=jnp.int32)
-    offset = position[:, None] - position[None, :]
-    allowed = (segments[:, None] == segments[None, :]) & (offset >= 0) & (offset < WINDOW)
-    weights = jnp.where(allowed, jnp.exp(scores), 0.0)
-    sink_terms = jnp.exp(sink_logits).reshape(key_rows.shape[1], -1)[:, :, None]
-    running = sink_terms + jnp.sum(weights, axis=-1)
-    attn_probs = (weights / running[..., None]).astype(jnp.bfloat16)
-    attended = jnp.einsum(
-        "grtu,ugd->tgrd", attn_probs, value_rows, preferred_element_type=jnp.float32
-    )
-    return attended.astype(jnp.bfloat16).reshape(row_count, -1)
-
-
-def gate_values(logits, choices, experts):
-    picked = choices[:, :, None] == jnp.arange(experts, dtype=jnp.int32)[None, None, :]
-    chosen = jnp.sum(jnp.where(picked, logits[:, None, :], 0.0), axis=-1)
-    raised = jnp.exp(chosen)
-    return raised / jnp.sum(raised, axis=-1, keepdims=True)
-
-
-def slot_numbers(choices, experts):
-    flat_ids = choices.reshape(-1)
-    onehot = (flat_ids[:, None] == jnp.arange(experts, dtype=jnp.int32)[None, :]).astype(jnp.int32)
-    earlier = jnp.cumsum(onehot, axis=0) - onehot
-    return jnp.sum(earlier * onehot, axis=1).reshape(choices.shape)
 
 
 def place():
@@ -275,10 +217,34 @@
     return (((y * 4 + z) * 4 + x) * 2 + core).reshape(-1)
 
 
-def dispatch_kernel(
-    rows, got, ring_rows, payload, picks, zsend, zrecv, send_sem, recv_sem
+PARTS = ((0, 768), (768, 768), (1536, 768), (2304, 640))
+
+
+def close_kernel(
+    heads,
+    o_full,
+    tokens_t,
+    ids,
+    router,
+    bias,
+    gain,
+    got,
+    rows,
+    total,
+    partial,
+    landed,
+    ring_rows,
+    payload,
+    picks,
+    psend,
+    precv,
+    zsend,
+    zrecv,
+    send_sem,
+    recv_sem,
 ):
-    _, y, z, x, core = place()
+    e, y, z, x, core = place()
+    group = lax.axis_index("dp")
     here = y * 8 + x * 2 + core
     above, below = expert_at(y, step(z, 1), x, core), expert_at(y, step(z, 3), x, core)
 
@@ -286,6 +252,8 @@
         return lax.div(index, 8) * 32 + z * 8 + lax.rem(index, 8)
 
     barrier = pltpu.get_barrier_semaphore()
+    other = {"dp": 1 - group, "expert": e}
+    pl.semaphore_signal(barrier, inc=1, device_id=other, device_id_type=MESH)
     for peer in (above, below):
         pl.semaphore_signal(barrier, inc=1, device_id={"expert": peer}, device_id_type=MESH)
 
@@ -295,7 +263,79 @@
         return carry
 
     lax.fori_loop(1, 32, signal_one, 0)
-    pl.semaphore_wait(barrier, 33)
+    pl.semaphore_wait(barrier, 34)
+
+    block, tail_tile = 128, pl.ds(META, 128)
+    mine = pl.ds(pl.multiple_of(group * block, block), block)
+    theirs = pl.ds(pl.multiple_of((1 - group) * block, block), block)
+    partial[:, tail_tile] = jnp.zeros((block, 128), jnp.bfloat16)
+    total[:, tail_tile] = jnp.zeros((block, 128), jnp.float32)
+    exchanges = []
+    for n, (start, lanes_here) in enumerate(PARTS):
+        inside = pl.ds(start, min(lanes_here, WIDTH - start))
+        update = jnp.dot(heads[theirs, :], o_full[:, inside], preferred_element_type=jnp.float32)
+        partial[:, inside] = update.astype(jnp.bfloat16)
+        lanes = pl.ds(start, lanes_here)
+        copy = pltpu.make_async_remote_copy(
+            src_ref=partial.at[:, lanes],
+            dst_ref=landed.at[:, lanes],
+            send_sem=psend.at[n],
+            recv_sem=precv.at[n],
+            device_id=other,
+            device_id_type=MESH,
+        )
+        copy.start()
+        exchanges.append(copy)
+    for start, lanes_here in PARTS:
+        inside = pl.ds(start, min(lanes_here, WIDTH - start))
+        total[:, inside] = jnp.dot(
+            heads[mine, :], o_full[:, inside], preferred_element_type=jnp.float32
+        )
+    for start in range(0, WIDTH, 128):
+        inside = pl.ds(start, min(128, WIDTH - start))
+        total[:, inside] = total[:, inside] + tokens_t[inside, mine].astype(jnp.float32).T
+
+    number = lax.broadcasted_iota(jnp.int32, (block, 128), 1)
+    row_number = lax.broadcasted_iota(jnp.int32, (block, 128), 0)
+    choices = ids[mine, :]
+    chosen = [(choices[:, k : k + 1] == number).astype(jnp.float32) for k in range(4)]
+    named = (chosen[0] + chosen[1] + chosen[2] + chosen[3]).astype(jnp.bfloat16)
+    earlier = jnp.dot(
+        (number < row_number).astype(jnp.bfloat16), named, preferred_element_type=jnp.float32
+    )
+    extra = jnp.zeros((block, 128), jnp.float32)
+    for k in range(4):
+        pick = choices[:, k : k + 1]
+        slot = jnp.sum(chosen[k] * earlier, axis=1, keepdims=True)
+        code = ((pick >> 5) * 64 + (pick & 7) * 8).astype(jnp.float32) + slot
+        extra = jnp.where(number == 68 + k, pick.astype(jnp.float32), extra)
+        extra = jnp.where(number == 72 + k, code, extra)
+        extra = jnp.where(number == 76 + k, ((pick >> 3) & 3).astype(jnp.float32), extra)
+
+    square = jnp.zeros((block, 1), jnp.float32)
+    for copy, (start, lanes_here) in zip(exchanges, PARTS):
+        copy.wait_recv()
+        lanes = pl.ds(start, lanes_here)
+        residual = total[:, lanes] + landed[:, lanes].astype(jnp.float32)
+        total[:, lanes] = residual
+        square = square + jnp.sum(residual * residual, axis=1, keepdims=True)
+    scale = lax.rsqrt(square * (1.0 / WIDTH) + norm_eps)
+    logits = bias[...] + jnp.zeros((block, 128), jnp.float32)
+    for start, lanes_here in PARTS:
+        lanes = pl.ds(start, lanes_here)
+        inside = pl.ds(start, min(lanes_here, WIDTH - start))
+        rows[:, lanes] = (total[:, lanes] * scale * gain[:, lanes]).astype(jnp.bfloat16)
+        logits = logits + jnp.dot(
+            rows[:, inside], router[inside, :], preferred_element_type=jnp.float32
+        )
+    raised = [
+        jnp.exp(jnp.sum(jnp.where(chosen[k] > 0.0, logits, 0.0), axis=1, keepdims=True))
+        for k in range(4)
+    ]
+    norm = raised[0] + raised[1] + raised[2] + raised[3]
+    for k in range(4):
+        extra = jnp.where(number == 64 + k, raised[k] / norm, extra)
+    rows[:, tail_tile] = rows[:, tail_tile] + extra.astype(jnp.bfloat16)
 
     meta = pl.ds(META, 128)
     chunks = ((0, 768), (768, 768), (1536, 768), (2304, 512))
@@ -381,28 +421,149 @@
     pltpu.make_async_copy(got, got, recv_sem).wait()
     part = payload.at[:, pl.ds(0, 31)]
     pltpu.make_async_copy(part, part, send_sem).wait()
-    for copy in (low_meta, high_meta, far_meta) + legs[5]:
+    for copy in (low_meta, high_meta, far_meta, *legs[5], *exchanges):
         copy.wait_send()
 
 
-def dispatch_rows(rows):
+def close(heads, o_full, tokens_t, ids, router, bias, gain):
     return pl.pallas_call(
-        dispatch_kernel,
+        close_kernel,
         out_shape=jax.ShapeDtypeStruct((128, 8, WIDE), jnp.bfloat16),
-        in_specs=[pl.BlockSpec(memory_space=pltpu.VMEM)],
+        in_specs=[pl.BlockSpec(memory_space=pltpu.VMEM)] * 7,
         out_specs=pl.BlockSpec(memory_space=pl.ANY),
         scratch_shapes=[
+            pltpu.VMEM((128, WIDE), jnp.bfloat16),
+            pltpu.VMEM((128, WIDE), jnp.float32),
+            pltpu.VMEM((128, WIDE), jnp.bfloat16),
+            pltpu.VMEM((128, WIDE), jnp.bfloat16),
             pltpu.VMEM((3, 128, WIDE), jnp.bfloat16),
             pltpu.VMEM((4, 32, 8, WIDE), jnp.bfloat16),
             pltpu.VMEM((4, 256, 128), jnp.bfloat16),
+            pltpu.SemaphoreType.DMA((4,)),
+            pltpu.SemaphoreType.DMA((4,)),
             pltpu.SemaphoreType.DMA((15,)),
             pltpu.SemaphoreType.DMA((15,)),
             pltpu.SemaphoreType.DMA,
             pltpu.SemaphoreType.DMA,
         ],
-        compiler_params=pltpu.CompilerParams(collective_id=1, has_side_effects=True),
-        name="dispatch_rows",
-    )(rows)
+        compiler_params=pltpu.CompilerParams(
+            collective_id=1, has_side_effects=True, vmem_limit_bytes=60 * 1024 * 1024
+        ),
+        name="close",
+    )(heads, o_full, tokens_t, ids, router, bias, gain)
+
+
+def attend_kernel(
+    qkv_eight,
+    qkv_two,
+    tokens_t,
+    gain,
+    segments,
+    sinks,
+    cosine,
+    sine,
+    heads,
+    weights,
+    normed,
+    from_eight,
+    from_two,
+    projected,
+    attended,
+    sem,
+):
+    fetch = pltpu.make_async_copy(qkv_eight, weights, sem)
+    fetch.start()
+    order = gathered_experts()
+    square = jnp.zeros((1, 256), jnp.float32)
+    for start in range(0, WIDTH, 192):
+        chunk = tokens_t[start : start + 192].astype(jnp.float32)
+        square = square + jnp.sum(chunk * chunk, axis=0, keepdims=True)
+    scale = lax.rsqrt(square * (1.0 / WIDTH) + norm_eps)
+    for start in range(0, WIDTH, 128):
+        size = min(128, WIDTH - start)
+        column = jnp.broadcast_to(gain[:, start : start + size], (128, size)).T
+        for half in range(2):
+            lanes = slice(half * 128, half * 128 + 128)
+            chunk = tokens_t[start : start + size, lanes].astype(jnp.float32)
+            normed[start : start + size, lanes] = (chunk * scale[:, lanes] * column).astype(
+                jnp.bfloat16
+            )
+    from_two[...] = jnp.dot(qkv_two[...], normed[...], preferred_element_type=jnp.float32)
+    fetch.wait()
+    for start in range(0, 1024, 256):
+        from_eight[start : start + 256] = jnp.dot(
+            weights[start : start + 256], normed[...], preferred_element_type=jnp.float32
+        )
+    for g in range(128):
+        row = int(order[g]) * 10
+        projected[row : row + 8] = from_eight[g * 8 : g * 8 + 8]
+        projected[row + 8 : row + 10] = from_two[g * 2 : g * 2 + 2]
+
+    def turn(row):
+        first, second = projected[row : row + 32], projected[row + 32 : row + 64]
+        return jnp.concatenate(
+            [
+                first * cosine[...] - second * sine[...],
+                second * cosine[...] + first * sine[...],
+            ],
+            axis=0,
+        )
+
+    owner = segments[...]
+    other = jnp.concatenate(
+        [jnp.broadcast_to(owner[:, h * 128 : h * 128 + 128], (128, 128)).T for h in range(2)], axis=0
+    )
+    other = jnp.concatenate([other, other], axis=1)
+    behind = lax.broadcasted_iota(jnp.int32, (256, 256), 1) - lax.broadcasted_iota(
+        jnp.int32, (256, 256), 0
+    )
+    allowed = (other == owner) & (behind >= 0) & (behind < WINDOW)
+    allowed = allowed.astype(jnp.float32)
+    for kv in range(2):
+        keys = turn(1024 + kv * 64).T.astype(jnp.bfloat16)
+        values = projected[1152 + kv * 64 : 1216 + kv * 64].astype(jnp.bfloat16)
+        for h in range(kv * 8, kv * 8 + 8):
+            queries = turn(h * 64).astype(jnp.bfloat16)
+            scores = jnp.dot(keys, queries, preferred_element_type=jnp.float32)
+            shares = jnp.where(allowed > 0.0, jnp.exp(scores * HEAD_DIM**-0.5), 0.0)
+            running = jnp.exp(sinks[:, h : h + 1]) + jnp.sum(shares, axis=0, keepdims=True)
+            probs = (shares * (1.0 / running)).astype(jnp.bfloat16)
+            attended[h * 64 : h * 64 + 64] = jnp.dot(
+                values, probs, preferred_element_type=jnp.float32
+            )
+    for j in range(8):
+        cut = jnp.concatenate(
+            [
+                attended[int(order[g]) * 8 : int(order[g]) * 8 + 8]
+                for g in range(j * 16, j * 16 + 16)
+            ],
+            axis=0,
+        )
+        for half in range(2):
+            heads[half * 128 : half * 128 + 128, j * 128 : j * 128 + 128] = (
+                cut[:, half * 128 : half * 128 + 128].T.astype(jnp.bfloat16)
+            )
+
+
+def attend(qkv_eight, qkv_two, tokens_t, gain, segments, sinks, cosine, sine):
+    return pl.pallas_call(
+        attend_kernel,
+        out_shape=jax.ShapeDtypeStruct((256, 1024), jnp.bfloat16),
+        in_specs=[pl.BlockSpec(memory_space=pl.ANY)]
+        + [pl.BlockSpec(memory_space=pltpu.VMEM)] * 7,
+        out_specs=pl.BlockSpec(memory_space=pltpu.VMEM),
+        scratch_shapes=[
+            pltpu.VMEM((1024, WIDTH), jnp.bfloat16),
+            pltpu.VMEM((WIDTH, 256), jnp.bfloat16),
+            pltpu.VMEM((1024, 256), jnp.float32),
+            pltpu.VMEM((256, 256), jnp.float32),
+            pltpu.VMEM((1280, 256), jnp.float32),
+            pltpu.VMEM((1024, 256), jnp.float32),
+            pltpu.SemaphoreType.DMA,
+        ],
+        compiler_params=pltpu.CompilerParams(vmem_limit_bytes=48 * 1024 * 1024),
+        name="attend",
+    )(qkv_eight, qkv_two, tokens_t, gain, segments, sinks, cosine, sine)
 
 
 def finish_kernel(got, out, gates):
@@ -448,14 +609,6 @@
         ],
         name="finish",
     )(got)
-
-
-def sent_and_summed(shard, axis, dim):
-    devices = lax.axis_size(axis)
-    before, after = (shard.shape[:dim], shard.shape[dim + 1 :])
-    blocks = jnp.moveaxis(shard.reshape(*before, devices, -1, *after), dim, 0)
-    tiles = lax.all_to_all(blocks, axis, 0, 0, tiled=True)
-    return jnp.sum(tiles.astype(jnp.float32), axis=0)
 
 
 def on_device(
@@ -477,82 +630,31 @@
     mlp_gain,
 ):
     tok_rows = tokens.shape[0]
-    groups = lax.axis_size("dp")
-    half_rows = tok_rows // groups
-    group_index = lax.axis_index("dp")
-    heads_here = sinks.shape[0]
-    kv_here = KV_HEADS * heads_here // HEADS
-    repeat_count = heads_here // kv_here
-    q_rows = heads_here * HEAD_DIM
-    kv_rows = kv_here * HEAD_DIM
     qkv_local = adam_weights(qkv_master, qkv_mom, qkv_var, qkv_grad)
     o_local = adam_weights(o_master, o_mom, o_var, o_grad)
     qkv_eight, qkv_two, o_full = gather_weights(qkv_local[:8], qkv_local[8:], o_local)
-    order = gathered_experts()
-    qkv_order = np.concatenate(
-        [
-            (order[:, None] * 10 + np.arange(8)[None, :]).reshape(-1),
-            (order[:, None] * 10 + np.arange(8, 10)[None, :]).reshape(-1),
-        ]
-    ).astype(np.int32)
-    o_order = (order[:, None] * 8 + np.arange(8)[None, :]).reshape(-1).astype(np.int32)
-    normed = rms_scale(tokens.astype(jnp.float32), attn_gain).astype(jnp.bfloat16)
-    qkv_eight = qkv_eight.reshape(-1, WIDTH)
-    qkv_two = qkv_two.reshape(-1, WIDTH)
-    shuffled = jnp.concatenate(
-        [
-            lax.dot_general(normed, w, contract_rows, preferred_element_type=jnp.float32)
-            for w in (qkv_eight, qkv_two)
-        ],
-        axis=1,
-    )
-    high = lax.reduce_precision(shuffled, 8, 7)
-    parts = jnp.concatenate([high, shuffled - high], axis=0).astype(jnp.bfloat16)
-    width_here = q_rows + 2 * kv_rows
-    unshuffle = (
-        jnp.asarray(qkv_order)[:, None] == jnp.arange(width_here, dtype=jnp.int32)[None, :]
-    ).astype(jnp.bfloat16)
-    both = jnp.dot(parts, unshuffle, preferred_element_type=jnp.float32)
-    projected = both[:tok_rows] + both[tok_rows:]
     positions = jnp.arange(tok_rows).astype(jnp.float32)
-    queries = rotate(
-        projected[:, :q_rows].reshape(tok_rows, heads_here, HEAD_DIM), positions
-    ).astype(jnp.bfloat16)
-    queries = queries.reshape(tok_rows, kv_here, repeat_count, HEAD_DIM)
-    key_rows = rotate(
-        projected[:, q_rows : q_rows + kv_rows].reshape(tok_rows, kv_here, HEAD_DIM), positions
-    ).astype(jnp.bfloat16)
-    value_rows = (
-        projected[:, q_rows + kv_rows :].reshape(tok_rows, kv_here, HEAD_DIM).astype(jnp.bfloat16)
-    )
-    attended = attention(queries, key_rows, value_rows, segment_ids, sinks)
-    shuffle = (
-        jnp.arange(q_rows, dtype=jnp.int32)[:, None] == jnp.asarray(o_order)[None, :]
-    ).astype(jnp.bfloat16)
-    attended = jnp.dot(attended, shuffle, preferred_element_type=jnp.float32).astype(jnp.bfloat16)
-    update = jnp.dot(attended, o_full.reshape(-1, WIDTH), preferred_element_type=jnp.float32)
-    summed = sent_and_summed(update.astype(jnp.bfloat16), "dp", 0)
-    own_rows = lax.dynamic_slice_in_dim(tokens, group_index * half_rows, half_rows, 0)
-    own_choices = lax.dynamic_slice_in_dim(expert_ids, group_index * half_rows, half_rows, 0)
-    residual = own_rows.astype(jnp.float32) + summed
-    moe_in = rms_scale(residual, mlp_gain).astype(jnp.bfloat16)
-    logits = jnp.dot(moe_in, router_weight, preferred_element_type=jnp.float32) + router_bias
-    experts = router_weight.shape[1]
-    gate_vals = gate_values(logits, own_choices, experts).astype(jnp.bfloat16)
-    slots = slot_numbers(own_choices, experts)
-    code = (own_choices // 32 * 8 + own_choices % 8) * 8 + slots
-    plane = own_choices // 8 % 4
-    extra = jnp.concatenate(
-        [
-            gate_vals,
-            own_choices.astype(jnp.bfloat16),
-            code.astype(jnp.bfloat16),
-            plane.astype(jnp.bfloat16),
-            jnp.zeros((half_rows, WIDE - WIDTH - 16), jnp.bfloat16),
-        ],
-        axis=1,
-    )
-    got = dispatch_rows(jnp.concatenate([moe_in, extra], axis=1))
+    spread = jnp.arange(HEAD_DIM // 2).astype(jnp.float32) * 2.0 / HEAD_DIM
+    angles = (rope_base**-spread)[:, None] * positions[None, :]
+    heads = attend(
+        qkv_eight.reshape(-1, WIDTH),
+        qkv_two.reshape(-1, WIDTH),
+        tokens.T,
+        attn_gain[None, :],
+        segment_ids.astype(jnp.float32)[None, :],
+        sinks[None, :],
+        jnp.cos(angles),
+        jnp.sin(angles),
+    )
+    got = close(
+        heads,
+        o_full.reshape(-1, WIDTH),
+        tokens.T,
+        expert_ids,
+        router_weight,
+        router_bias[None, :],
+        jnp.pad(mlp_gain, (0, WIDE - WIDTH))[None, :],
+    )
     dispatched, gates = finish(got)
     dispatched = jnp.transpose(dispatched, (2, 0, 1))[None, :, None]
     gates = jnp.transpose(gates).astype(jnp.bfloat16)[None, :, None]

time: 206 us -> 197 us (0.956)
  Pallas kernels: 144 us -> 181 us
  matrix products: 15.6 us -> 0 us
  waiting for transfers between devices: 14.5 us -> 0 us
  local copies, waits for them, and re-layouts: 17.1 us -> 9.66 us
  starting transfers between devices: 4.01 us -> 0 us
  other arithmetic: 8.57 us -> 5.2 us
    pallas_call x1 -> x2, Pallas kernels: 76.1 us -> 113 us  [the longest x1 103 us: close(): pl.pallas_call(close_kernel, out_shape=jax.ShapeDtypeStruct((128, 8, WIDE...]
    dot_general x7 -> x0, matrix products: 15.6 us -> none  [the longest x1 5.88 us: on_device(): jnp.dot(attended, o_full.reshape(-1, WIDTH), preferred_element_type=jnp.f...]
    all_to_all x1 -> x0, waiting for transfers between devices: 14.5 us -> none  [sent_and_summed(): tiles = lax.all_to_all(blocks, axis, 0, 0, tiled=True)]
    all_to_all x1 -> x0, starting transfers between devices: 4.01 us -> none  [sent_and_summed(): tiles = lax.all_to_all(blocks, axis, 0, 0, tiled=True)]
    reduce_sum x6 -> x0, other arithmetic: 2.55 us -> none  [the longest x1 1.35 us: sent_and_summed(): return jnp.sum(tiles.astype(jnp.float32), axis=0)]
    reshape x3 -> x1, local copies, waits for them, and re-layouts: 5.74 us -> 3.49 us  [on_device(): qkv_two.reshape(-1, WIDTH)]
  transfers between devices with their start and end apart: 1 -> 0, of which waited for: 1 -> 0; matrix products, arithmetic and copies ran while one was open for 2% -> 0% of each run, Pallas kernels for 0% -> 0%
where the time goes in v3:
time: 197 us
  Pallas kernels  181 us (92%)
  local copies, waits for them, and re-layouts  9.66 us (5%)
  other arithmetic  5.2 us (3%)
    pallas_call x1, Pallas kernels, close(): pl.pallas_call(close_kernel, out_shape=jax.ShapeDtypeStruct((128, 8, WIDE...  103 us
    pallas_call x1, Pallas kernels, gather_weights(): pl.pallas_call(gather_kernel, out_shape=[jax.ShapeDtypeStruct((2, 4, 4, 4...  60.1 us
    pallas_call x1, Pallas kernels, attend(): pl.pallas_call(attend_kernel, out_shape=jax.ShapeDtypeStruct((256, 1024),...  9.59 us
    pallas_call x1, Pallas kernels, finish(): pl.pallas_call(finish_kernel, grid=(-(-WIDE // FINISH_LANES),), out_shape...  8.11 us

profile of v3, /device:TPU:1, one launch (start us, length us, event | category | flops | bytes accessed | tf_op | source)
XLA Modules:
  0.0 196.9 jit_solution(17715815558080828900)
XLA Ops:
  0.6 1.3 fusion.7
  2.0 0.6 slice.8.a
  2.6 0.6 slice.9.b
  3.2 1.7 fusion.15.o
  4.9 60.1 %gather_weights.1 = (bf16[2,4,4,4,8,2880]{5,4,3,2,1,0:T(8,128)(2,1)}, bf16[2,4,4,4,2,2880]{5,4,3,2,1,0:T(2,128)(2,1)}, bf16[2,4,4,4,8,2880]{5,4,3,2,1,0:T(8,128)(2,1)}) custom-call(bf16[8,2880]{1,0:T(8,128)(2,1)} %slice.8.a, bf16[2,2880]{1,0:T(2,128)(2,1)} %slice.9.b, bf16[8,2880]{1,0:T(8,128)(2,1)} %fusion.15.o), custom_call_target="tpu_custom_call" | custom-call | tf_op jit(solution)/shard_map/gather_weights/pallas_call | solution.py:194
  65.0 0.0 copy-start.4
  65.0 0.0 copy-start.3
  65.1 3.5 %reshape.25.qkv_two = bf16[256,2880]{1,0:T(8,128)(2,1)S(1)} reshape(bf16[2,4,4,4,2,2880]{5,4,3,2,1,0:T(2,128)(2,1)} %get-tuple-element.8) | data formatting | bytes 2949120 | tf_op jit(solution)/shard_map/reshape | solution.py:641
  68.6 0.2 multiply_sine_fusion
  68.8 0.7 broadcast_in_dim.23.gain
  69.5 0.7 convert_element_type.37
  70.2 0.0 copy-start
  70.2 1.4 copy-done
  71.6 0.0 copy-start.2
  71.6 0.7 copy-done.2
  72.2 9.6 %attend.1.heads = bf16[256,1024]{1,0:T(8,128)(2,1)S(1)} custom-call(bf16[1024,2880]{1,0:T(8,128)(2,1)} %bitcast.18, bf16[256,2880]{1,0:T(8,128)(2,1)S(1)} %reshape.25.qkv_two, bf16[2880,256]{1,0:T(8,128)(2,1)S(1)} %bitcast.14, f32[1,2880]{1,0:T(1,128)S(1)} %broadcast_in_dim.23.gain, f32[1,256]{1,0:T(1,128)S(1)} %bitcast.15, f32[1,16]{1,0:T(1,128)S(1)} %bitcast.16, ...), custom_call_target="tpu_custom_call" | custom-call | tf_op jit(solution)/shard_map/attend/pallas_call | solution.py:549
  81.8 0.0 copy-start.1
  81.8 0.8 copy-done.1
  82.6 0.0 copy-done.4
  82.6 0.8 copy.19.ids
  83.4 0.0 copy-done.3
  83.4 0.6 broadcast_in_dim.27.gain
  84.0 103.5 %close.1.got = bf16[128,8,2944]{2,1,0:T(8,128)(2,1)} custom-call(bf16[256,1024]{1,0:T(8,128)(2,1)} %copy-done.1, bf16[1024,2880]{1,0:T(8,128)(2,1)} %bitcast.17, bf16[2880,256]{1,0:T(8,128)(2,1)} %bitcast.13, s32[256,4]{1,0:T(8,128)} %copy.19.ids, bf16[2880,128]{1,0:T(8,128)(2,1)} %router.1, f32[1,128]{1,0:T(1,128)} %bitcast.19, f32[1,2944]{1,0:T(1,128)} %broadcast_in_dim.27.gain), custom_call_target="tpu_custom_call" | custom-call | tf_op jit(solution)/shard_map/close/pallas_call | solution.py:429
  187.5 8.1 %finish.1 = (bf16[8,2880,128]{2,1,0:T(8,128)(2,1)}, f32[8,128]{1,0:T(8,128)}) custom-call(bf16[128,8,2944]{2,1,0:T(8,128)(2,1)} %close.1.got), custom_call_target="tpu_custom_call" | custom-call | tf_op jit(solution)/shard_map/finish/pallas_call | solution.py:598
  195.6 1.2 convert_bitcast_fusion
  (3 shorter events, 0.0 us)
Async XLA Ops:
  65.0 17.6 %copy-start.4 = (s32[256,4]{0,1:T(4,128)S(1)}, s32[256,4]{0,1:T(4,128)}, u32[]{:S(2)}) copy-start(s32[256,4]{0,1:T(4,128)} %param.18) | copy-start | bytes 12292
  65.0 18.4 %copy-start.3 = (f32[2880]{0:T(1024)S(1)}, f32[2880]{0:T(1024)}, u32[]{:S(2)}) copy-start(f32[2880]{0:T(1024)} %param.31) | copy-start | bytes 34564
  70.2 1.4 copy-start
  71.6 0.7 copy-start.2
  81.8 0.8 copy-start.1

commit v4 on v3

--- a/solution.py
+++ b/solution.py
@@ -13,7 +13,6 @@
 HALF = 1408
 META = 2816
 MESH = pl.DeviceIdType.MESH
-GATHER_SPACE = pl.ANY
 FINISH_LANES = 768
 
 beta_one = 0.9
@@ -69,7 +68,40 @@
     )
 
 
-def gather_kernel(a, b, o, ga, gb, go, send, recv, local):
+def gathered_experts():
+    core, last, middle, z = np.meshgrid(
+        np.arange(2), np.arange(4), np.arange(4), np.arange(4), indexing="ij"
+    )
+    y = np.where(core == 0, middle, last)
+    x = np.where(core == 0, last, middle)
+    return (((y * 4 + z) * 4 + x) * 2 + core).reshape(-1)
+
+
+def open_kernel(
+    a,
+    b,
+    o,
+    tokens,
+    gain,
+    segments,
+    sinks,
+    cosine,
+    sine,
+    go,
+    heads,
+    tokens_t,
+    ga,
+    gb,
+    normed,
+    from_eight,
+    from_two,
+    two_rows,
+    projected,
+    attended,
+    send,
+    recv,
+    local,
+):
     _, y, z, x, core = place()
     middle = y * (1 - core) + x * core
     last = x * (1 - core) + y * core
@@ -91,6 +123,8 @@
     greet([p for pair in ring for p in pair] + [partner])
     streams = ((a, ga), (b, gb), (o, go))
     copies = {}
+    fetch = pltpu.make_async_copy(tokens, tokens_t, local.at[3])
+    fetch.start()
 
     def move(s, tag, src, dst, to):
         k = sum(1 for key in copies if key[0] == s)
@@ -154,67 +188,177 @@
         block = full.at[core, last, middle]
         move(s, "middle up", block, block, ring[1][0])
         move(s, "middle down", block, block, ring[1][1])
-        if s != 1:
+        if s == 0:
             along_last(s, 0)
     for s, (_, full) in enumerate(streams):
         arrived(s, "middle up")
         block = full.at[core, last, step(middle, 3), pl.ds(0, 2)]
         move(s, "middle far 0", block, block, ring[1][0])
-        if s != 1:
+        if s == 0:
             along_last(s, 1)
         arrived(s, "middle down")
         block = full.at[core, last, step(middle, 1), pl.ds(2, 2)]
         move(s, "middle far 1", block, block, ring[1][1])
-        if s != 1:
+        if s == 0:
             along_last(s, 2)
     for s in range(3):
         arrived(s, "middle far 0")
-        if s != 1:
+        if s == 0:
             along_last(s, 3)
         arrived(s, "middle far 1")
-        along_last(s, 4 if s != 1 else 0)
+        if s < 2:
+            along_last(s, 4 if s == 0 else 0)
+    fetch.wait()
+    square = jnp.zeros((1, 256), jnp.float32)
+    for start in range(0, WIDTH, 192):
+        chunk = tokens_t[start : start + 192].astype(jnp.float32)
+        square = square + jnp.sum(chunk * chunk, axis=0, keepdims=True)
+    scale = lax.rsqrt(square * (1.0 / WIDTH) + norm_eps)
+    for start in range(0, WIDTH, 128):
+        size = min(128, WIDTH - start)
+        column = jnp.broadcast_to(gain[0:1, start : start + size], (128, size)).T
+        for half in range(2):
+            lanes = slice(half * 128, half * 128 + 128)
+            chunk = tokens_t[start : start + size, lanes].astype(jnp.float32)
+            normed[start : start + size, lanes] = (chunk * scale[:, lanes] * column).astype(
+                jnp.bfloat16
+            )
     for k in range(5):
-        for s in range(3):
-            if k < len(pieces[s]):
-                from_last(s, k)
+        from_last(0, k)
+        if k == 0:
+            from_last(1, 0)
+        if k >= 2:
+            along_last(2, k - 2)
+    along_last(2, 3)
+    along_last(2, 4)
+
+    def from_far(s, k):
+        block = part(s, 2, k)
+        arrived(s, ("far", k))
+        move(s, ("pair", 2, k), block, block, partner)
+
     for k in range(5):
-        for s in range(3):
-            if k < len(pieces[s]):
-                block = part(s, 2, k)
-                arrived(s, ("far", k))
-                move(s, ("pair", 2, k), block, block, partner)
+        from_far(0, k)
+    from_far(1, 0)
+
+    def output_step(n):
+        if n < 5:
+            from_last(2, n)
+        elif n < 10:
+            from_far(2, n - 5)
+
     for (s, tag), copy in copies.items():
-        if tag[0] == "pair":
+        if s < 2 and tag[0] == "pair":
+            copy.wait_recv()
+    output_step(0)
+    order = gathered_experts()
+    for n in range(128):
+        two = gb[n // 64, n // 16 % 4, n // 4 % 4, n % 4]
+        two_rows[n * 2 : n * 2 + 2] = two.astype(jnp.float32)
+    output_step(1)
+    from_two[...] = jnp.dot(
+        two_rows[...].astype(jnp.bfloat16), normed[...], preferred_element_type=jnp.float32
+    )
+    for n in range(4):
+        rows = ga[n // 2, n % 2 * 2 : n % 2 * 2 + 2].reshape(256, WIDTH)
+        from_eight[n * 256 : n * 256 + 256] = jnp.dot(
+            rows, normed[...], preferred_element_type=jnp.float32
+        )
+        if n % 2 == 1:
+            output_step(2 + n // 2)
+    for g in range(128):
+        row = int(order[g]) * 10
+        projected[row : row + 8] = from_eight[g * 8 : g * 8 + 8]
+        projected[row + 8 : row + 10] = from_two[g * 2 : g * 2 + 2]
+    output_step(4)
+
+    def turn(row):
+        first, second = projected[row : row + 32], projected[row + 32 : row + 64]
+        return jnp.concatenate(
+            [
+                first * cosine[...] - second * sine[...],
+                second * cosine[...] + first * sine[...],
+            ],
+            axis=0,
+        )
+
+    owner = segments[...].astype(jnp.float32)
+    other = jnp.concatenate(
+        [jnp.broadcast_to(owner[:, h * 128 : h * 128 + 128], (128, 128)).T for h in range(2)], axis=0
+    )
+    other = jnp.concatenate([other, other], axis=1)
+    behind = lax.broadcasted_iota(jnp.int32, (256, 256), 1) - lax.broadcasted_iota(
+        jnp.int32, (256, 256), 0
+    )
+    allowed = (other == owner) & (behind >= 0) & (behind < WINDOW)
+    allowed = allowed.astype(jnp.float32)
+    for kv in range(2):
+        keys = turn(1024 + kv * 64).T.astype(jnp.bfloat16)
+        values = projected[1152 + kv * 64 : 1216 + kv * 64].astype(jnp.bfloat16)
+        for h in range(kv * 8, kv * 8 + 8):
+            if h % 4 == 0:
+                output_step(h // 4 + 5)
+            queries = turn(h * 64).astype(jnp.bfloat16)
+            scores = jnp.dot(keys, queries, preferred_element_type=jnp.float32)
+            shares = jnp.where(allowed > 0.0, jnp.exp(scores * HEAD_DIM**-0.5), 0.0)
+            running = jnp.exp(sinks[:, h : h + 1]) + jnp.sum(shares, axis=0, keepdims=True)
+            probs = (shares * (1.0 / running)).astype(jnp.bfloat16)
+            attended[h * 64 : h * 64 + 64] = jnp.dot(
+                values, probs, preferred_element_type=jnp.float32
+            )
+    output_step(9)
+    for j in range(8):
+        cut = jnp.concatenate(
+            [
+                attended[int(order[g]) * 8 : int(order[g]) * 8 + 8]
+                for g in range(j * 16, j * 16 + 16)
+            ],
+            axis=0,
+        )
+        for half in range(2):
+            heads[half * 128 : half * 128 + 128, j * 128 : j * 128 + 128] = (
+                cut[:, half * 128 : half * 128 + 128].T.astype(jnp.bfloat16)
+            )
+    for (s, tag), copy in copies.items():
+        if s == 2 and tag[0] == "pair":
             copy.wait_recv()
     for copy in copies.values():
         copy.wait_send()
 
 
-def gather_weights(a, b, o):
+def open_up(a, b, o, tokens_t, gain, segments, sinks, cosine, sine):
     return pl.pallas_call(
-        gather_kernel,
+        open_kernel,
         out_shape=[
-            jax.ShapeDtypeStruct((2, 4, 4, 4) + v.shape, jnp.bfloat16) for v in (a, b, o)
+            jax.ShapeDtypeStruct((2, 4, 4, 4, 8, WIDTH), jnp.bfloat16),
+            jax.ShapeDtypeStruct((256, 1024), jnp.bfloat16),
         ],
-        in_specs=[pl.BlockSpec(memory_space=pltpu.VMEM)] * 3,
-        out_specs=[pl.BlockSpec(memory_space=GATHER_SPACE)] * 3,
+        in_specs=[pl.BlockSpec(memory_space=pltpu.VMEM)] * 3
+        + [pl.BlockSpec(memory_space=pltpu.HBM)]
+        + [pl.BlockSpec(memory_space=pltpu.VMEM)] * 5,
+        out_specs=[
+            pl.BlockSpec(memory_space=pl.ANY),
+            pl.BlockSpec(memory_space=pltpu.VMEM),
+        ],
         scratch_shapes=[
+            pltpu.VMEM((WIDTH, 256), jnp.bfloat16),
+            pltpu.VMEM((2, 4, 4, 4, 8, WIDTH), jnp.bfloat16),
+            pltpu.VMEM((2, 4, 4, 4, 2, WIDTH), jnp.bfloat16),
+            pltpu.VMEM((WIDTH, 256), jnp.bfloat16),
+            pltpu.VMEM((1024, 256), jnp.float32),
+            pltpu.VMEM((256, 256), jnp.float32),
+            pltpu.VMEM((256, WIDTH), jnp.float32),
+            pltpu.VMEM((1280, 256), jnp.float32),
+            pltpu.VMEM((1024, 256), jnp.float32),
             pltpu.SemaphoreType.DMA((3, 42)),
             pltpu.SemaphoreType.DMA((3, 42)),
-            pltpu.SemaphoreType.DMA((3,)),
+            pltpu.SemaphoreType.DMA((4,)),
         ],
-        compiler_params=pltpu.CompilerParams(collective_id=0, has_side_effects=True),
-        name="gather_weights",
-    )(a, b, o)
-
-
-def gathered_experts():
-    core, last, middle, z = np.meshgrid(
-        np.arange(2), np.arange(4), np.arange(4), np.arange(4), indexing="ij"
-    )
-    y = np.where(core == 0, middle, last)
-    x = np.where(core == 0, last, middle)
-    return (((y * 4 + z) * 4 + x) * 2 + core).reshape(-1)
+        compiler_params=pltpu.CompilerParams(
+            collective_id=0, has_side_effects=True, vmem_limit_bytes=60 * 1024 * 1024
+        ),
+        name="open",
+    )(a, b, o, tokens_t, gain, segments, sinks, cosine, sine)
 
 
 PARTS = ((0, 768), (768, 768), (1536, 768), (2304, 640))
@@ -222,13 +366,15 @@
 
 def close_kernel(
     heads,
-    o_full,
-    tokens_t,
+    o_there,
+    tokens,
     ids,
     router,
     bias,
     gain,
     got,
+    o_full,
+    tokens_t,
     rows,
     total,
     partial,
@@ -242,7 +388,14 @@
     zrecv,
     send_sem,
     recv_sem,
+    local,
 ):
+    fetches = [
+        pltpu.make_async_copy(src, dst, local.at[k])
+        for k, (src, dst) in enumerate(((o_there, o_full), (tokens, tokens_t)))
+    ]
+    for copy in fetches:
+        copy.start()
     e, y, z, x, core = place()
     group = lax.axis_index("dp")
     here = y * 8 + x * 2 + core
@@ -271,6 +424,7 @@
     partial[:, tail_tile] = jnp.zeros((block, 128), jnp.bfloat16)
     total[:, tail_tile] = jnp.zeros((block, 128), jnp.float32)
     exchanges = []
+    fetches[0].wait()
     for n, (start, lanes_here) in enumerate(PARTS):
         inside = pl.ds(start, min(lanes_here, WIDTH - start))
         update = jnp.dot(heads[theirs, :], o_full[:, inside], preferred_element_type=jnp.float32)
@@ -291,26 +445,26 @@
         total[:, inside] = jnp.dot(
             heads[mine, :], o_full[:, inside], preferred_element_type=jnp.float32
         )
+    fetches[1].wait()
     for start in range(0, WIDTH, 128):
         inside = pl.ds(start, min(128, WIDTH - start))
         total[:, inside] = total[:, inside] + tokens_t[inside, mine].astype(jnp.float32).T
 
     number = lax.broadcasted_iota(jnp.int32, (block, 128), 1)
     row_number = lax.broadcasted_iota(jnp.int32, (block, 128), 0)
-    choices = ids[mine, :]
-    chosen = [(choices[:, k : k + 1] == number).astype(jnp.float32) for k in range(4)]
+    chosen = [(ids[k : k + 1, mine] == row_number).astype(jnp.float32).T for k in range(4)]
     named = (chosen[0] + chosen[1] + chosen[2] + chosen[3]).astype(jnp.bfloat16)
     earlier = jnp.dot(
         (number < row_number).astype(jnp.bfloat16), named, preferred_element_type=jnp.float32
     )
+    expert = number.astype(jnp.float32)
+    first_slot = ((number >> 5) * 64 + (number & 7) * 8).astype(jnp.float32) + earlier
+    plane_of = ((number >> 3) & 3).astype(jnp.float32)
     extra = jnp.zeros((block, 128), jnp.float32)
     for k in range(4):
-        pick = choices[:, k : k + 1]
-        slot = jnp.sum(chosen[k] * earlier, axis=1, keepdims=True)
-        code = ((pick >> 5) * 64 + (pick & 7) * 8).astype(jnp.float32) + slot
-        extra = jnp.where(number == 68 + k, pick.astype(jnp.float32), extra)
-        extra = jnp.where(number == 72 + k, code, extra)
-        extra = jnp.where(number == 76 + k, ((pick >> 3) & 3).astype(jnp.float32), extra)
+        for at, what in ((68, expert), (72, first_slot), (76, plane_of)):
+            value = jnp.sum(chosen[k] * what, axis=1, keepdims=True)
+            extra = jnp.where(number == at + k, value, extra)
 
     square = jnp.zeros((block, 1), jnp.float32)
     for copy, (start, lanes_here) in zip(exchanges, PARTS):
@@ -322,9 +476,8 @@
     scale = lax.rsqrt(square * (1.0 / WIDTH) + norm_eps)
     logits = bias[...] + jnp.zeros((block, 128), jnp.float32)
     for start, lanes_here in PARTS:
-        lanes = pl.ds(start, lanes_here)
         inside = pl.ds(start, min(lanes_here, WIDTH - start))
-        rows[:, lanes] = (total[:, lanes] * scale * gain[:, lanes]).astype(jnp.bfloat16)
+        rows[:, inside] = (total[:, inside] * scale * gain[:, inside]).astype(jnp.bfloat16)
         logits = logits + jnp.dot(
             rows[:, inside], router[inside, :], preferred_element_type=jnp.float32
         )
@@ -335,7 +488,9 @@
     norm = raised[0] + raised[1] + raised[2] + raised[3]
     for k in range(4):
         extra = jnp.where(number == 64 + k, raised[k] / norm, extra)
-    rows[:, tail_tile] = rows[:, tail_tile] + extra.astype(jnp.bfloat16)
+    rows[:, tail_tile] = jnp.where(
+        number < WIDTH - META, rows[:, tail_tile].astype(jnp.float32), extra
+    ).astype(jnp.bfloat16)
 
     meta = pl.ds(META, 128)
     chunks = ((0, 768), (768, 768), (1536, 768), (2304, 512))
@@ -429,9 +584,13 @@
     return pl.pallas_call(
         close_kernel,
         out_shape=jax.ShapeDtypeStruct((128, 8, WIDE), jnp.bfloat16),
-        in_specs=[pl.BlockSpec(memory_space=pltpu.VMEM)] * 7,
+        in_specs=[pl.BlockSpec(memory_space=pltpu.VMEM)]
+        + [pl.BlockSpec(memory_space=pltpu.HBM)] * 2
+        + [pl.BlockSpec(memory_space=pltpu.VMEM)] * 4,
         out_specs=pl.BlockSpec(memory_space=pl.ANY),
         scratch_shapes=[
+            pltpu.VMEM((1024, WIDTH), jnp.bfloat16),
+            pltpu.VMEM((WIDTH, 256), jnp.bfloat16),
             pltpu.VMEM((128, WIDE), jnp.bfloat16),
             pltpu.VMEM((128, WIDE), jnp.float32),
             pltpu.VMEM((128, WIDE), jnp.bfloat16),
@@ -445,125 +604,13 @@
             pltpu.SemaphoreType.DMA((15,)),
             pltpu.SemaphoreType.DMA,
             pltpu.SemaphoreType.DMA,
+            pltpu.SemaphoreType.DMA((2,)),
         ],
         compiler_params=pltpu.CompilerParams(
             collective_id=1, has_side_effects=True, vmem_limit_bytes=60 * 1024 * 1024
         ),
         name="close",
     )(heads, o_full, tokens_t, ids, router, bias, gain)
-
-
-def attend_kernel(
-    qkv_eight,
-    qkv_two,
-    tokens_t,
-    gain,
-    segments,
-    sinks,
-    cosine,
-    sine,
-    heads,
-    weights,
-    normed,
-    from_eight,
-    from_two,
-    projected,
-    attended,
-    sem,
-):
-    fetch = pltpu.make_async_copy(qkv_eight, weights, sem)
-    fetch.start()
-    order = gathered_experts()
-    square = jnp.zeros((1, 256), jnp.float32)
-    for start in range(0, WIDTH, 192):
-        chunk = tokens_t[start : start + 192].astype(jnp.float32)
-        square = square + jnp.sum(chunk * chunk, axis=0, keepdims=True)
-    scale = lax.rsqrt(square * (1.0 / WIDTH) + norm_eps)
-    for start in range(0, WIDTH, 128):
-        size = min(128, WIDTH - start)
-        column = jnp.broadcast_to(gain[:, start : start + size], (128, size)).T
-        for half in range(2):
-            lanes = slice(half * 128, half * 128 + 128)
-            chunk = tokens_t[start : start + size, lanes].astype(jnp.float32)
-            normed[start : start + size, lanes] = (chunk * scale[:, lanes] * column).astype(
-                jnp.bfloat16
-            )
-    from_two[...] = jnp.dot(qkv_two[...], normed[...], preferred_element_type=jnp.float32)
-    fetch.wait()
-    for start in range(0, 1024, 256):
-        from_eight[start : start + 256] = jnp.dot(
-            weights[start : start + 256], normed[...], preferred_element_type=jnp.float32
-        )
-    for g in range(128):
-        row = int(order[g]) * 10
-        projected[row : row + 8] = from_eight[g * 8 : g * 8 + 8]
-        projected[row + 8 : row + 10] = from_two[g * 2 : g * 2 + 2]
-
-    def turn(row):
-        first, second = projected[row : row + 32], projected[row + 32 : row + 64]
-        return jnp.concatenate(
-            [
-                first * cosine[...] - second * sine[...],
-                second * cosine[...] + first * sine[...],
-            ],
-            axis=0,
-        )
-
-    owner = segments[...]
-    other = jnp.concatenate(
-        [jnp.broadcast_to(owner[:, h * 128 : h * 128 + 128], (128, 128)).T for h in range(2)], axis=0
-    )
-    other = jnp.concatenate([other, other], axis=1)
-    behind = lax.broadcasted_iota(jnp.int32, (256, 256), 1) - lax.broadcasted_iota(
-        jnp.int32, (256, 256), 0
-    )
-    allowed = (other == owner) & (behind >= 0) & (behind < WINDOW)
-    allowed = allowed.astype(jnp.float32)
-    for kv in range(2):
-        keys = turn(1024 + kv * 64).T.astype(jnp.bfloat16)
-        values = projected[1152 + kv * 64 : 1216 + kv * 64].astype(jnp.bfloat16)
-        for h in range(kv * 8, kv * 8 + 8):
-            queries = turn(h * 64).astype(jnp.bfloat16)
-            scores = jnp.dot(keys, queries, preferred_element_type=jnp.float32)
-            shares = jnp.where(allowed > 0.0, jnp.exp(scores * HEAD_DIM**-0.5), 0.0)
-            running = jnp.exp(sinks[:, h : h + 1]) + jnp.sum(shares, axis=0, keepdims=True)
-            probs = (shares * (1.0 / running)).astype(jnp.bfloat16)
-            attended[h * 64 : h * 64 + 64] = jnp.dot(
-                values, probs, preferred_element_type=jnp.float32
-            )
-    for j in range(8):
-        cut = jnp.concatenate(
-            [
-                attended[int(order[g]) * 8 : int(order[g]) * 8 + 8]
-                for g in range(j * 16, j * 16 + 16)
-            ],
-            axis=0,
-        )
-        for half in range(2):
-            heads[half * 128 : half * 128 + 128, j * 128 : j * 128 + 128] = (
-                cut[:, half * 128 : half * 128 + 128].T.astype(jnp.bfloat16)
-            )
-
-
-def attend(qkv_eight, qkv_two, tokens_t, gain, segments, sinks, cosine, sine):
-    return pl.pallas_call(
-        attend_kernel,
-        out_shape=jax.ShapeDtypeStruct((256, 1024), jnp.bfloat16),
-        in_specs=[pl.BlockSpec(memory_space=pl.ANY)]
-        + [pl.BlockSpec(memory_space=pltpu.VMEM)] * 7,
-        out_specs=pl.BlockSpec(memory_space=pltpu.VMEM),
-        scratch_shapes=[
-            pltpu.VMEM((1024, WIDTH), jnp.bfloat16),
-            pltpu.VMEM((WIDTH, 256), jnp.bfloat16),
-            pltpu.VMEM((1024, 256), jnp.float32),
-            pltpu.VMEM((256, 256), jnp.float32),
-            pltpu.VMEM((1280, 256), jnp.float32),
-            pltpu.VMEM((1024, 256), jnp.float32),
-            pltpu.SemaphoreType.DMA,
-        ],
-        compiler_params=pltpu.CompilerParams(vmem_limit_bytes=48 * 1024 * 1024),
-        name="attend",
-    )(qkv_eight, qkv_two, tokens_t, gain, segments, sinks, cosine, sine)
 
 
 def finish_kernel(got, out, gates):
@@ -588,10 +635,12 @@
     def _():
         mine = lax.axis_index("expert").astype(jnp.float32)
         first = WIDTH % FINISH_LANES
+        found = []
         for c in range(8):
             data = whole[c][first : first + 8]
             asked = jnp.where(data[4:8] == mine, data[:4], 0.0)
-            gates[c : c + 1] = jnp.sum(asked, axis=0, keepdims=True)
+            found.append(jnp.sum(asked, axis=0, keepdims=True))
+        gates[...] = jnp.concatenate(found, axis=0).astype(jnp.bfloat16)
 
 
 def finish(got):
@@ -600,7 +649,7 @@
         grid=(-(-WIDE // FINISH_LANES),),
         out_shape=[
             jax.ShapeDtypeStruct((8, WIDTH, 128), jnp.bfloat16),
-            jax.ShapeDtypeStruct((8, 128), jnp.float32),
+            jax.ShapeDtypeStruct((8, 128), jnp.bfloat16),
         ],
         in_specs=[pl.BlockSpec((128, 8, FINISH_LANES), lambda i: (0, 0, i))],
         out_specs=[
@@ -632,16 +681,16 @@
     tok_rows = tokens.shape[0]
     qkv_local = adam_weights(qkv_master, qkv_mom, qkv_var, qkv_grad)
     o_local = adam_weights(o_master, o_mom, o_var, o_grad)
-    qkv_eight, qkv_two, o_full = gather_weights(qkv_local[:8], qkv_local[8:], o_local)
     positions = jnp.arange(tok_rows).astype(jnp.float32)
     spread = jnp.arange(HEAD_DIM // 2).astype(jnp.float32) * 2.0 / HEAD_DIM
     angles = (rope_base**-spread)[:, None] * positions[None, :]
-    heads = attend(
-        qkv_eight.reshape(-1, WIDTH),
-        qkv_two.reshape(-1, WIDTH),
+    o_full, heads = open_up(
+        qkv_local[:8],
+        qkv_local[8:],
+        o_local,
         tokens.T,
         attn_gain[None, :],
-        segment_ids.astype(jnp.float32)[None, :],
+        segment_ids[None, :],
         sinks[None, :],
         jnp.cos(angles),
         jnp.sin(angles),
@@ -650,14 +699,14 @@
         heads,
         o_full.reshape(-1, WIDTH),
         tokens.T,
-        expert_ids,
+        expert_ids.T,
         router_weight,
         router_bias[None, :],
-        jnp.pad(mlp_gain, (0, WIDE - WIDTH))[None, :],
+        mlp_gain[None, :],
     )
     dispatched, gates = finish(got)
     dispatched = jnp.transpose(dispatched, (2, 0, 1))[None, :, None]
-    gates = jnp.transpose(gates).astype(jnp.bfloat16)[None, :, None]
+    gates = jnp.transpose(gates)[None, :, None]
     return (dispatched, gates)
 
 

time: 197 us -> 183 us (0.929)
  Pallas kernels: 181 us -> 174 us
  local copies, waits for them, and re-layouts: 9.66 us -> 3.86 us
    pallas_call x1, Pallas kernels: 103 us -> 98.2 us  [close(): pl.pallas_call(close_kernel, out_shape=jax.ShapeDtypeStruct((128, 8, WIDE...]
    unnamed x11 -> x0, local copies, waits for them, and re-layouts: 3.62 us -> none
    reshape x1 -> x0, local copies, waits for them, and re-layouts: 3.49 us -> none  [on_device(): qkv_two.reshape(-1, WIDTH)]
    pallas_call x2 -> x1, Pallas kernels: 69.7 us -> 68 us  [open_up(): pl.pallas_call(open_kernel, out_shape=[jax.ShapeDtypeStruct((2, 4, 4, 4,...]
where the time goes in v4:
time: 183 us
  Pallas kernels  174 us (95%)
  other arithmetic  3.91 us (2%)
  local copies, waits for them, and re-layouts  3.86 us (2%)
    pallas_call x1, Pallas kernels, close(): pl.pallas_call(close_kernel, out_shape=jax.ShapeDtypeStruct((128, 8, WIDE...  98.2 us
    pallas_call x1, Pallas kernels, open_up(): pl.pallas_call(open_kernel, out_shape=[jax.ShapeDtypeStruct((2, 4, 4, 4,...  68 us
    pallas_call x1, Pallas kernels, finish(): pl.pallas_call(finish_kernel, grid=(-(-WIDE // FINISH_LANES),), out_shape...  8.12 us

profile of v4, /device:TPU:1, one launch (start us, length us, event | category | flops | bytes accessed | tf_op | source)
XLA Modules:
  0.0 182.8 jit_solution(6297261311264487358)
XLA Ops:
  0.7 1.3 broadcast_in_dim.23.gain
  2.0 1.3 broadcast_in_dim.27.gain
  3.3 1.7 fusion.15.o
  5.0 0.8 multiply_sine_fusion
  5.8 1.3 fusion.7
  7.2 0.6 slice.9.b
  7.8 0.6 slice.8.a
  8.4 68.0 %open.1 = (bf16[2,4,4,4,8,2880]{5,4,3,2,1,0:T(8,128)(2,1)}, bf16[256,1024]{1,0:T(8,128)(2,1)}) custom-call(bf16[8,2880]{1,0:T(8,128)(2,1)} %slice.8.a, bf16[2,2880]{1,0:T(2,128)(2,1)} %slice.9.b, bf16[8,2880]{1,0:T(8,128)(2,1)} %fusion.15.o, bf16[2880,256]{1,0:T(8,128)(2,1)} %bitcast.13, f32[1,2880]{1,0:T(1,128)} %broadcast_in_dim.23.gain, ...), custom_call_target="tpu_custom_call" | custom-call | tf_op jit(solution)/shard_map/open/pallas_call | solution.py:330
  76.4 98.2 %close.1.got = bf16[128,8,2944]{2,1,0:T(8,128)(2,1)} custom-call(bf16[256,1024]{1,0:T(8,128)(2,1)} %get-tuple-element.6.heads, bf16[1024,2880]{1,0:T(8,128)(2,1)} %bitcast.12, bf16[2880,256]{1,0:T(8,128)(2,1)} %bitcast.14, s32[4,256]{1,0:T(4,128)} %bitcast.15, bf16[2880,128]{1,0:T(8,128)(2,1)} %router.1, f32[1,128]{1,0:T(1,128)} %bitcast.17, ...), custom_call_target="tpu_custom_call" | custom-call | tf_op jit(solution)/shard_map/close/pallas_call | solution.py:584
  174.7 8.1 %finish.1 = (bf16[8,2880,128]{2,1,0:T(8,128)(2,1)}, bf16[8,128]{1,0:T(8,128)(2,1)}) custom-call(bf16[128,8,2944]{2,1,0:T(8,128)(2,1)} %close.1.got), custom_call_target="tpu_custom_call" | custom-call | tf_op jit(solution)/shard_map/finish/pallas_call | solution.py:647
  (2 shorter events, 0.0 us)

commit v5 on v4

--- a/solution.py
+++ b/solution.py
@@ -30,7 +30,7 @@
     fix_one = 1.0 - beta_one**adam_step
     fix_two = 1.0 - beta_two**adam_step
     update = moment_new / fix_one / (jnp.sqrt(second_new / fix_two) + adam_eps)
-    return (master - learn_rate * update).astype(jnp.bfloat16)
+    return master - learn_rate * update
 
 
 def place():
@@ -78,9 +78,14 @@
 
 
 def open_kernel(
-    a,
-    b,
-    o,
+    qkv_state,
+    qkv_mom,
+    qkv_var,
+    qkv_grad,
+    o_state,
+    o_mom,
+    o_var,
+    o_grad,
     tokens,
     gain,
     segments,
@@ -89,6 +94,9 @@
     sine,
     go,
     heads,
+    a,
+    b,
+    o,
     tokens_t,
     ga,
     gb,
@@ -120,6 +128,16 @@
         (peer(last, step(middle, 1), z), peer(last, step(middle, 3), z)),
         (peer(step(last, 1), middle, z), peer(step(last, 3), middle, z)),
     ]
+    for start in range(0, WIDTH, 640):
+        lanes = slice(start, min(start + 640, WIDTH))
+        updated = adam_weights(
+            qkv_state[:, lanes], qkv_mom[:, lanes], qkv_var[:, lanes], qkv_grad[:, lanes]
+        )
+        a[:, lanes] = updated[:8].astype(jnp.bfloat16)
+        b[:, lanes] = updated[8:].astype(jnp.bfloat16)
+        o[:, lanes] = adam_weights(
+            o_state[:, lanes], o_mom[:, lanes], o_var[:, lanes], o_grad[:, lanes]
+        ).astype(jnp.bfloat16)
     greet([p for pair in ring for p in pair] + [partner])
     streams = ((a, ga), (b, gb), (o, go))
     copies = {}
@@ -326,14 +344,14 @@
         copy.wait_send()
 
 
-def open_up(a, b, o, tokens_t, gain, segments, sinks, cosine, sine):
+def open_up(*operands):
     return pl.pallas_call(
         open_kernel,
         out_shape=[
             jax.ShapeDtypeStruct((2, 4, 4, 4, 8, WIDTH), jnp.bfloat16),
             jax.ShapeDtypeStruct((256, 1024), jnp.bfloat16),
         ],
-        in_specs=[pl.BlockSpec(memory_space=pltpu.VMEM)] * 3
+        in_specs=[pl.BlockSpec(memory_space=pltpu.VMEM)] * 8
         + [pl.BlockSpec(memory_space=pltpu.HBM)]
         + [pl.BlockSpec(memory_space=pltpu.VMEM)] * 5,
         out_specs=[
@@ -341,6 +359,9 @@
             pl.BlockSpec(memory_space=pltpu.VMEM),
         ],
         scratch_shapes=[
+            pltpu.VMEM((8, WIDTH), jnp.bfloat16),
+            pltpu.VMEM((2, WIDTH), jnp.bfloat16),
+            pltpu.VMEM((8, WIDTH), jnp.bfloat16),
             pltpu.VMEM((WIDTH, 256), jnp.bfloat16),
             pltpu.VMEM((2, 4, 4, 4, 8, WIDTH), jnp.bfloat16),
             pltpu.VMEM((2, 4, 4, 4, 2, WIDTH), jnp.bfloat16),
@@ -358,7 +379,7 @@
             collective_id=0, has_side_effects=True, vmem_limit_bytes=60 * 1024 * 1024
         ),
         name="open",
-    )(a, b, o, tokens_t, gain, segments, sinks, cosine, sine)
+    )(*operands)
 
 
 PARTS = ((0, 768), (768, 768), (1536, 768), (2304, 640))
@@ -466,6 +487,16 @@
             value = jnp.sum(chosen[k] * what, axis=1, keepdims=True)
             extra = jnp.where(number == at + k, value, extra)
 
+    def choose(block, data):
+        code = lax.broadcasted_iota(jnp.int32, (128, 256), 1).astype(jnp.float32)
+        plane = z.astype(jnp.float32)
+        hit = jnp.zeros((128, 256), jnp.float32)
+        for k in range(4):
+            same = (data[:, 72 + k : 73 + k] == code) & (data[:, 76 + k : 77 + k] == plane)
+            hit = hit + jnp.where(same, 1.0, 0.0)
+        picks[block] = hit.T.astype(jnp.bfloat16)
+
+    choose(0, extra)
     square = jnp.zeros((block, 1), jnp.float32)
     for copy, (start, lanes_here) in zip(exchanges, PARTS):
         copy.wait_recv()
@@ -474,23 +505,28 @@
         total[:, lanes] = residual
         square = square + jnp.sum(residual * residual, axis=1, keepdims=True)
     scale = lax.rsqrt(square * (1.0 / WIDTH) + norm_eps)
-    logits = bias[...] + jnp.zeros((block, 128), jnp.float32)
     for start, lanes_here in PARTS:
         inside = pl.ds(start, min(lanes_here, WIDTH - start))
         rows[:, inside] = (total[:, inside] * scale * gain[:, inside]).astype(jnp.bfloat16)
-        logits = logits + jnp.dot(
-            rows[:, inside], router[inside, :], preferred_element_type=jnp.float32
-        )
-    raised = [
-        jnp.exp(jnp.sum(jnp.where(chosen[k] > 0.0, logits, 0.0), axis=1, keepdims=True))
-        for k in range(4)
-    ]
-    norm = raised[0] + raised[1] + raised[2] + raised[3]
-    for k in range(4):
-        extra = jnp.where(number == 64 + k, raised[k] / norm, extra)
-    rows[:, tail_tile] = jnp.where(
-        number < WIDTH - META, rows[:, tail_tile].astype(jnp.float32), extra
-    ).astype(jnp.bfloat16)
+
+    def route():
+        logits = bias[...] + jnp.zeros((block, 128), jnp.float32)
+        for start, lanes_here in PARTS:
+            inside = pl.ds(start, min(lanes_here, WIDTH - start))
+            logits = logits + jnp.dot(
+                rows[:, inside], router[inside, :], preferred_element_type=jnp.float32
+            )
+        raised = [
+            jnp.exp(jnp.sum(jnp.where(chosen[k] > 0.0, logits, 0.0), axis=1, keepdims=True))
+            for k in range(4)
+        ]
+        norm = raised[0] + raised[1] + raised[2] + raised[3]
+        whole = extra
+        for k in range(4):
+            whole = jnp.where(number == 64 + k, raised[k] / norm, whole)
+        rows[:, tail_tile] = jnp.where(
+            number < WIDTH - META, rows[:, tail_tile].astype(jnp.float32), whole
+        ).astype(jnp.bfloat16)
 
     meta = pl.ds(META, 128)
     chunks = ((0, 768), (768, 768), (1536, 768), (2304, 512))
@@ -512,19 +548,7 @@
             down = pass_on(2 * n + 1, from_high, 2, pl.ds(*chunks[7 - n]), below)
         return up, down
 
-    low_meta = pass_on(12, rows, 0, meta, above)
-    high_meta = pass_on(13, rows, 1, meta, below)
     legs = [leg(0)]
-
-    def choose(block, source):
-        data = source[:, META:WIDE].astype(jnp.float32)
-        code = lax.broadcasted_iota(jnp.int32, (128, 256), 1).astype(jnp.float32)
-        plane = z.astype(jnp.float32)
-        hit = jnp.zeros((128, 256), jnp.float32)
-        for k in range(4):
-            same = (data[:, 72 + k : 73 + k] == code) & (data[:, 76 + k : 77 + k] == plane)
-            hit = hit + jnp.where(same, 1.0, 0.0)
-        picks[block] = hit.T.astype(jnp.bfloat16)
 
     def deliver(block, source, z_at, chunk):
         start, lanes_here = chunks[chunk]
@@ -552,14 +576,17 @@
 
         lax.fori_loop(1, 32, one, 0)
 
-    choose(0, rows)
-    for chunk in range(4):
+    deliver(0, rows, z, 0)
+    route()
+    low_meta = pass_on(12, rows, 0, meta, above)
+    high_meta = pass_on(13, rows, 1, meta, below)
+    for chunk in range(1, 4):
         deliver(0, rows, z, chunk)
     low_meta.wait_recv()
     far_meta = pass_on(14, from_low, 2, meta, above)
     high_meta.wait_recv()
-    choose(1, from_low)
-    choose(2, from_high)
+    choose(1, from_low[:, META:WIDE].astype(jnp.float32))
+    choose(2, from_high[:, META:WIDE].astype(jnp.float32))
     for n in range(6):
         up, down = legs[n]
         if n < 5:
@@ -568,7 +595,7 @@
             legs.append(leg(n + 1))
         if n == 3:
             far_meta.wait_recv()
-            choose(3, from_far)
+            choose(3, from_far[:, META:WIDE].astype(jnp.float32))
         up.wait_recv()
         deliver(*((1, from_low, step(z, 3), n) if n < 4 else (3, from_far, step(z, 2), n - 4)))
         down.wait_recv()
@@ -617,11 +644,11 @@
     spot = pl.program_id(0)
     lanes_here = got.shape[2]
     halves = []
+    source = lax.broadcasted_iota(jnp.int32, (512, 512), 0)
+    target = lax.broadcasted_iota(jnp.int32, (512, 512), 1)
+    pick = (source == (target & 63) * 8 + (target >> 6)).astype(jnp.bfloat16)
     for part in range(2):
         rows = got[part * 64 : part * 64 + 64].reshape(512, lanes_here)
-        source = lax.broadcasted_iota(jnp.int32, (512, 512), 0)
-        target = lax.broadcasted_iota(jnp.int32, (512, 512), 1)
-        pick = (source == (target & 63) * 8 + (target >> 6)).astype(jnp.bfloat16)
         halves.append(
             lax.dot_general(rows, pick, (((0,), (0,)), ((), ())), preferred_element_type=jnp.float32)
         )
@@ -679,15 +706,18 @@
     mlp_gain,
 ):
     tok_rows = tokens.shape[0]
-    qkv_local = adam_weights(qkv_master, qkv_mom, qkv_var, qkv_grad)
-    o_local = adam_weights(o_master, o_mom, o_var, o_grad)
     positions = jnp.arange(tok_rows).astype(jnp.float32)
     spread = jnp.arange(HEAD_DIM // 2).astype(jnp.float32) * 2.0 / HEAD_DIM
     angles = (rope_base**-spread)[:, None] * positions[None, :]
     o_full, heads = open_up(
-        qkv_local[:8],
-        qkv_local[8:],
-        o_local,
+        qkv_master,
+        qkv_mom,
+        qkv_var,
+        qkv_grad,
+        o_master,
+        o_mom,
+        o_var,
+        o_grad,
         tokens.T,
         attn_gain[None, :],
         segment_ids[None, :],

time: 183 us -> 180 us (0.984)
  other arithmetic: 3.91 us -> 0.85 us
  Pallas kernels: 174 us -> 176 us
    convert_element_type x2 -> x0, other arithmetic: 3.08 us -> none  [adam_weights(): return (master - learn_rate * update).astype(jnp.bfloat16)]
where the time goes in v5:
time: 180 us
  Pallas kernels  176 us (98%)
  local copies, waits for them, and re-layouts  2.63 us (1%)
    pallas_call x1, Pallas kernels, close(): pl.pallas_call(close_kernel, out_shape=jax.ShapeDtypeStruct((128, 8, WIDE...  99 us
    pallas_call x1, Pallas kernels, open_up(): pl.pallas_call(open_kernel, out_shape=[jax.ShapeDtypeStruct((2, 4, 4, 4,...  68.7 us
    pallas_call x1, Pallas kernels, finish(): pl.pallas_call(finish_kernel, grid=(-(-WIDE // FINISH_LANES),), out_shape...  8.11 us

profile of v5, /device:TPU:1, one launch (start us, length us, event | category | flops | bytes accessed | tf_op | source)
XLA Modules:
  0.0 180.0 jit_solution(6378158046476121782)
XLA Ops:
  0.7 1.3 broadcast_in_dim.23.gain
  2.0 1.3 broadcast_in_dim.27.gain
  3.3 0.8 multiply_sine_fusion
  4.1 68.7 %open.1 = (bf16[2,4,4,4,8,2880]{5,4,3,2,1,0:T(8,128)(2,1)}, bf16[256,1024]{1,0:T(8,128)(2,1)}) custom-call(f32[10,2880]{1,0:T(8,128)} %qkv_state.1, f32[10,2880]{1,0:T(8,128)} %qkv_mom.1, f32[10,2880]{1,0:T(8,128)} %qkv_var.1, f32[10,2880]{1,0:T(8,128)} %qkv_grad.1, f32[8,2880]{1,0:T(8,128)} %o_state.1, f32[8,2880]{1,0:T(8,128)} %o_mom.1, f32[8,2880]{1,0:T(8,128)} %o_var.1, ...), custom_call_target="tpu_custom_call" | custom-call | tf_op jit(solution)/shard_map/open/pallas_call | solution.py:348
  72.8 99.0 %close.1.got = bf16[128,8,2944]{2,1,0:T(8,128)(2,1)} custom-call(bf16[256,1024]{1,0:T(8,128)(2,1)} %get-tuple-element.6.heads, bf16[1024,2880]{1,0:T(8,128)(2,1)} %bitcast.12, bf16[2880,256]{1,0:T(8,128)(2,1)} %bitcast.14, s32[4,256]{1,0:T(4,128)} %bitcast.15, bf16[2880,128]{1,0:T(8,128)(2,1)} %router.1, f32[1,128]{1,0:T(1,128)} %bitcast.17, ...), custom_call_target="tpu_custom_call" | custom-call | tf_op jit(solution)/shard_map/close/pallas_call | solution.py:611
  171.8 8.1 %finish.1 = (bf16[8,2880,128]{2,1,0:T(8,128)(2,1)}, bf16[8,128]{1,0:T(8,128)(2,1)}) custom-call(bf16[128,8,2944]{2,1,0:T(8,128)(2,1)} %close.1.got), custom_call_target="tpu_custom_call" | custom-call | tf_op jit(solution)/shard_map/finish/pallas_call | solution.py:674
  (2 shorter events, 0.0 us)
